TPU v7x, 32 devices: a whole 2x2x4 slice. The times are simulated.
32 devices in a mesh: clip: 2 (over y), seq: 4 (over z), head: 4 (over x, core).
Axes of the slice: x: 2, y: 2, z: 4, core: 2. Of those that a mesh axis runs over, the one named last changes fastest.
Arguments:
- queries: bfloat16 [16, 4, 16, 3072], P(('clip', 'head'), 'seq'), parts along dimension 0, may hold values from -15 to 15
- attn_keys: bfloat16 [16, 4, 16, 3072], P(('clip', 'head'), 'seq'), parts along dimension 0, may hold values from -5 to 5
- attn_values: bfloat16 [16, 4, 16, 3072], P(('clip', 'head'), 'seq'), parts along dimension 0, may hold values from -5 to 5
- residual: bfloat16 [16, 4, 16, 5120], P(('clip', 'head'), 'seq'), parts along dimension 0, may hold values from -6 to 6
- out_weight: bfloat16 [3072, 5120], P('head', 'seq'), may hold values from -0.109375 to 0.109375
- out_gate: float32 [5120], replicated, may hold values from 0.3 to 3
- head_shift: float32 [5120], replicated, may hold values from -3 to 3
- head_scale: float32 [5120], replicated, may hold values from -1.5 to 1.5
- head_weight: bfloat16 [5120, 64], replicated, may hold values from -0.078125 to 0.078125
- head_bias: float32 [64], replicated, may hold values from -3 to 3
- conv_weight: bfloat16 [3, 3, 3, 16, 384], replicated, may hold values from -0.3125 to 0.3125
- conv_bias: float32 [384], replicated, may hold values from -3 to 3
- norm_gain: float32 [384], replicated, may hold values from 0.5 to 2
Outputs:
- hidden: bfloat16 [16, 4, 16, 5120], P(('clip', 'head'), 'seq'), parts along dimension 0
- features: bfloat16 [16, 8, 32, 384], P(('clip', 'head'), 'seq'), parts along dimension 0
There are 2 independent parts, one for each index of `clip`. A program takes and returns all parts, laid end to end along the dimension named above; an argument that names none is the same for every part. Nothing has to cross between parts.
All inputs are finite; a program needn't handle non-finite values.
Results may differ from a plain program's by a relative error of at most 0.013.
Values may be sent and summed in bfloat16 or wider, within the bound.
A program may use at most 128 MiB of HBM per device.

v0:
```python
import functools
import math

import jax
import jax.numpy as jnp
from jax import lax
from jax.experimental import pallas as pl
from jax.experimental.pallas import tpu as pltpu
from jax.sharding import PartitionSpec as P

HEAD_DIM = 128


def from_behind(value, axis, steps):
    count = lax.axis_size(axis)
    first, last = (max(0, -steps), min(count, count - steps))
    return lax.ppermute(value, axis, [(source, source + steps) for source in range(first, last)])


def padded_2(x, sides, width):
    for axis, dim in sides:
        peers, length = (lax.axis_size(axis), x.shape[dim])
        up = [(i, (i + 1) % peers) for i in range(peers - 1)]
        down = [(j, i) for i, j in up]
        last = lax.slice_in_dim(x, length - width, length, axis=dim)
        first = lax.slice_in_dim(x, 0, width, axis=dim)
        before = lax.ppermute(last, axis, up)
        after = lax.ppermute(first, axis, down)
        x = jnp.concatenate([before, x, after], axis=dim)
    return x


def head_latent(hidden, head_shift, head_scale, head_weight, head_bias):
    values = hidden.astype(jnp.float32)
    center = values - jnp.mean(values, -1, keepdims=True)
    spread = jnp.mean(center * center, -1, keepdims=True)
    normed = (center * lax.rsqrt(spread + 1e-06) * (1.0 + head_scale) + head_shift).astype(
        jnp.bfloat16
    )
    flat = normed.reshape(-1, normed.shape[-1])
    latent = (jnp.dot(flat, head_weight, preferred_element_type=jnp.float32) + head_bias).astype(
        jnp.bfloat16
    )
    frames, height, breadth = (hidden.shape[0], hidden.shape[1], hidden.shape[2])
    channels = head_weight.shape[1] // 4
    patches = latent.reshape(frames, height, breadth, 2, 2, channels).transpose(0, 1, 3, 2, 4, 5)
    return patches.reshape(frames, height * 2, breadth * 2, channels)


def convolve(padded, frames, conv_weight, conv_bias, norm_gain):
    height = padded.shape[1] - 2
    breadth = padded.shape[2] - 2
    stacked = jnp.concatenate(
        [
            padded[
                time_off : time_off + frames,
                row_off : row_off + height,
                col_off : col_off + breadth,
            ]
            for time_off in range(3)
            for row_off in range(3)
            for col_off in range(3)
        ],
        -1,
    )
    kernel = conv_weight.reshape(-1, conv_weight.shape[-1])
    linear = (
        jnp.dot(stacked.reshape(-1, stacked.shape[-1]), kernel, preferred_element_type=jnp.float32)
        + conv_bias
    )
    normed = linear * lax.rsqrt(jnp.mean(linear * linear, -1, keepdims=True) + 1e-06) * norm_gain
    return jax.nn.silu(normed).astype(jnp.bfloat16).reshape(frames, height, breadth, -1)


def attend_block(carried, block_keys, block_values, query_heads):
    running, denominator, weighted = carried
    scores = jnp.einsum("hqd,khd->hqk", query_heads, block_keys, preferred_element_type=jnp.float32)
    scores = scores * query_heads.shape[-1] ** (-0.5)
    newmax = jnp.maximum(running, jnp.max(scores, -1))
    factor = jnp.exp(running - newmax)
    weights = jnp.exp(scores - newmax[..., None])
    denominator = denominator * factor + jnp.sum(weights, -1)
    product = jnp.einsum(
        "hqk,khd->hqd",
        weights.astype(jnp.bfloat16),
        block_values,
        preferred_element_type=jnp.float32,
    )
    weighted = weighted * factor[..., None] + product
    return (newmax, denominator, weighted)


def fold_pieces(query_heads, carried, pieces):
    key_piece, value_piece = pieces
    frames, height, breadth = (key_piece.shape[0], key_piece.shape[1], key_piece.shape[2])
    heads_here, head_width = (query_heads.shape[0], query_heads.shape[2])
    group_rows = 4

    def regroup(one_piece):
        shaped = one_piece.reshape(
            frames, height // group_rows, group_rows, breadth, heads_here, head_width
        )
        shaped = shaped.transpose(1, 0, 2, 3, 4, 5)
        return shaped.reshape(
            height // group_rows, frames * group_rows * breadth, heads_here, head_width
        )

    def advance(inner, blocks):
        return (attend_block(inner, blocks[0], blocks[1], query_heads), None)

    carried, _ = lax.scan(advance, carried, (regroup(key_piece), regroup(value_piece)))
    return carried


def on_device_gathered(
    queries,
    attn_keys,
    attn_values,
    residual,
    out_weight,
    out_gate,
    head_shift,
    head_scale,
    head_weight,
    head_bias,
    conv_weight,
    conv_bias,
    norm_gain,
):
    head_count = lax.axis_size("head")
    frames_dev = queries.shape[0]
    group_width = queries.shape[3] // head_count
    head_width = HEAD_DIM
    heads_here = group_width // head_width
    local_queries, local_keys, local_values = (
        lax.all_to_all(queries, "head", split_axis=3, concat_axis=0, tiled=True),
        lax.all_to_all(attn_keys, "head", split_axis=3, concat_axis=0, tiled=True),
        lax.all_to_all(attn_values, "head", split_axis=3, concat_axis=0, tiled=True),
    )
    frames_all, height, breadth = (
        local_queries.shape[0],
        local_queries.shape[1],
        local_queries.shape[2],
    )
    count = frames_all * height * breadth
    query_heads = local_queries.reshape(count, heads_here, head_width).transpose(1, 0, 2)
    initial = (
        jnp.full((heads_here, count), -1e30, jnp.float32),
        jnp.zeros((heads_here, count), jnp.float32),
        jnp.zeros((heads_here, count, head_width), jnp.float32),
    )
    carried = fold_pieces(
        query_heads,
        initial,
        (
            lax.all_gather(local_keys, "seq", axis=1, tiled=True),
            lax.all_gather(local_values, "seq", axis=1, tiled=True),
        ),
    )
    running, denominator, weighted = carried
    attended = (weighted / denominator[..., None]).astype(jnp.bfloat16)
    attended = attended.transpose(1, 0, 2).reshape(count, group_width)
    partial_value = jnp.dot(
        attended,
        lax.all_gather(out_weight, "seq", axis=1, tiled=True),
        preferred_element_type=jnp.float32,
    )
    partial_value = partial_value.reshape(frames_all, height, breadth, partial_value.shape[-1])
    owned = lax.psum_scatter(
        partial_value.astype(jnp.bfloat16), "head", scatter_dimension=0, tiled=True
    ).astype(jnp.float32)
    hidden = (residual.astype(jnp.float32) + out_gate * owned).astype(jnp.bfloat16)
    own_video = head_latent(hidden, head_shift, head_scale, head_weight, head_bias)
    earlier = from_behind(own_video, "head", 1)
    video = jnp.concatenate([earlier, own_video], 0)
    extended = padded_2(video, (("seq", 1),), 1)
    padded = jnp.pad(extended, ((0, 0), (0, 0), (1, 1), (0, 0)))
    features = convolve(padded, frames_dev, conv_weight, conv_bias, norm_gain)
    return (hidden, features)


MESH = pl.DeviceIdType.MESH


class Plan:
    def __init__(self, ns, nh, queries, residual, out_weight):
        self.ns, self.nh = ns, nh
        self.tokens = queries.shape[0] * queries.shape[1] * queries.shape[2]
        self.group = queries.shape[3] // nh // HEAD_DIM
        self.parts = ns // math.gcd(self.group, ns)
        self.units = self.group * self.parts // ns
        self.width = residual.shape[3]
        self.columns = out_weight.shape[1]
        self.slots = ns * nh
        self.chunk = 256 if self.columns % 256 == 0 else 128
        self.chunks = self.columns // self.chunk
        self.bits = nh.bit_length() - 1

    def fits(self, queries):
        return (
            self.nh == 1 << self.bits
            and self.bits == 2
            and self.ns % 2 == 0
            and self.parts == 2
            and self.units == 3
            and self.tokens % 16 == 0
            and self.columns % 128 == 0
            and queries.shape[0] >= 2
            and self.slots * self.tokens <= 1024
        )


def block_kernel(
    plan,
    q_hbm, k_hbm, v_hbm, res_hbm, w_hbm, hw_hbm,
    gate_ref, shift_ref, scale_ref, bias_ref,
    hidden_ref, near_ref,
    qkv, got, att, weight, res, head_w, term, *rest,
):
    p = plan
    landed = rest[: p.bits]
    final, patch, halo = rest[p.bits : p.bits + 3]
    (local_sem, own_sem, s1, r1, sf, rf, s3, r3, s5, r5, s6, r6, s7, r7) = rest[p.bits + 3 :]
    s = lax.axis_index("seq")
    h = lax.axis_index("head")
    here = s * p.nh + h

    loads = [
        pltpu.make_async_copy(q_hbm, qkv.at[0], local_sem.at[0]),
        pltpu.make_async_copy(k_hbm, qkv.at[1], local_sem.at[1]),
        pltpu.make_async_copy(v_hbm, qkv.at[2], local_sem.at[2]),
    ]
    late = [
        pltpu.make_async_copy(w_hbm, weight, local_sem.at[3]),
        pltpu.make_async_copy(res_hbm, res, local_sem.at[4]),
        pltpu.make_async_copy(hw_hbm, head_w, local_sem.at[5]),
    ]
    for copy in loads:
        copy.start()

    offsets = [(ds, dh) for ds in range(p.ns) for dh in range(p.nh) if ds or dh]
    barrier = pltpu.get_barrier_semaphore()
    for ds, dh in offsets:
        pl.semaphore_signal(
            barrier,
            inc=1,
            device_id={"seq": lax.rem(s + ds, p.ns), "head": lax.rem(h + dh, p.nh)},
            device_id_type=MESH,
        )
    for copy in loads:
        copy.wait()
    pl.semaphore_wait(barrier, len(offsets))

    def piece(seq_index, head_index, j):
        start = (head_index * p.group + 3 * (seq_index // 2) + seq_index % 2 + j) * HEAD_DIM
        return qkv.at[:, :, pl.ds(pl.multiple_of(start, HEAD_DIM), HEAD_DIM)]

    def place(seq_index, k):
        return 1 - seq_index % 2 if k == 0 else seq_index % 2

    def direct(source, target):
        up = (source // 2 < target // 2) & (target % 2 == 1)
        down = (source // 2 > target // 2) & (target % 2 == 0)
        return jnp.logical_not(up | down)

    def first_hop(index, k, to_s, to_h, slot, j):
        return pltpu.make_async_remote_copy(
            src_ref=piece(to_s, to_h, j),
            dst_ref=got.at[slot, j],
            send_sem=s1.at[index, k],
            recv_sem=r1.at[index, k],
            device_id={"seq": to_s, "head": to_h},
            device_id_type=MESH,
        )

    def sending(index, k):
        ds, dh = offsets[index]
        to_s, to_h = lax.rem(s + ds, p.ns), lax.rem(h + dh, p.nh)
        return to_s, first_hop(index, k, to_s, to_h, here, place(to_s, k))

    def arriving(index, k):
        ds, dh = offsets[index]
        from_s, from_h = lax.rem(s - ds + p.ns, p.ns), lax.rem(h - dh + p.nh, p.nh)
        return from_s, first_hop(index, k, s, h, from_s * p.nh + from_h, place(s, k))

    def guarded(k, ds, source, target, act):
        if k == 0 and ds:
            pl.when(direct(source, target))(act)
        else:
            act()

    for k in range(2):
        for index, (ds, dh) in enumerate(offsets):
            to_s, copy = sending(index, k)
            guarded(k, ds, s, to_s, copy.start)
    own = [
        pltpu.make_async_copy(piece(s, h, j), got.at[here, j], own_sem.at[j]) for j in range(2)
    ]
    for copy in own:
        copy.start()
    for copy in late:
        copy.start()
    for copy in own:
        copy.wait()

    even = s % 2 == 0
    peer_s = s + 1 - 2 * (s % 2)

    def hand_on(level, j_from, j_to):
        rows = pl.ds(level * p.nh, p.nh)
        return pltpu.make_async_remote_copy(
            src_ref=got.at[rows, j_from, pl.ds(1, 2)],
            dst_ref=got.at[rows, j_to, pl.ds(1, 2)],
            send_sem=sf.at[level],
            recv_sem=rf.at[level],
            device_id={"seq": peer_s},
            device_id_type=MESH,
        )

    def handed(level):
        return jnp.where(even, level // 2 < s // 2, level // 2 > s // 2)

    def expected(level):
        return jnp.where(even, level // 2 > s // 2, level // 2 < s // 2)

    for ds in list(range(1, p.ns)) + [0]:
        for index, (ds2, dh) in enumerate(offsets):
            if ds2 == ds:
                from_s, copy = arriving(index, 0)
                guarded(0, ds, from_s, s, copy.wait_recv)
        if ds:
            level = lax.rem(s - ds + p.ns, p.ns)

            @pl.when(handed(level))
            def _():
                hand_on(level, place(s, 0), place(peer_s, 0)).start()

    for index in range(len(offsets)):
        arriving(index, 1)[1].wait_recv()

    per_part = p.slots // p.parts

    def gather_hop(source, i, step):
        return pltpu.make_async_remote_copy(
            src_ref=att.at[source, i],
            dst_ref=att.at[source, i],
            send_sem=s3.at[(step + 1) // 2, source, i],
            recv_sem=r3.at[source, i],
            device_id={"seq": lax.rem(s + step + p.ns, p.ns)},
            device_id_type=MESH,
        )

    up_open, down_open = s + 1 < p.ns, s > 0
    for i in range(p.units):
        j = place(s, 1) if i < 2 else place(s, 0)
        part = i if i < 2 else s % 2
        if i == 2:
            for ds in range(1, p.ns):
                level = lax.rem(s - ds + p.ns, p.ns)

                @pl.when(expected(level))
                def _():
                    hand_on(level, place(peer_s, 0), place(s, 0)).wait_recv()

        q = got[pl.ds(part * per_part, per_part), j, 0].reshape(-1, HEAD_DIM)
        k = got[:, j, 1].reshape(-1, HEAD_DIM)
        v = got[:, j, 2].reshape(-1, HEAD_DIM)
        scores = lax.dot_general(
            q, k, (((1,), (1,)), ((), ())), preferred_element_type=jnp.float32
        )
        scores = scores * HEAD_DIM ** (-0.5)
        weights = jnp.exp(scores - jnp.max(scores, -1, keepdims=True))
        denominator = jnp.sum(weights, -1, keepdims=True)
        product = jnp.dot(weights.astype(jnp.bfloat16), v, preferred_element_type=jnp.float32)
        att[s, i] = (product / denominator).astype(jnp.bfloat16)
        pl.when(up_open)(gather_hop(s, i, 1).start)
        pl.when(down_open)(gather_hop(s, i, -1).start)

    late[0].wait()
    for distance in range(1, p.ns):
        for i in range(p.units):

            @pl.when(s - distance >= 0)
            def _():
                gather_hop(s - distance, i, 1).wait_recv()
                pl.when(up_open)(gather_hop(s - distance, i, 1).start)

            @pl.when(s + distance < p.ns)
            def _():
                gather_hop(s + distance, i, -1).wait_recv()
                pl.when(down_open)(gather_hop(s + distance, i, -1).start)

    def halving(c, b):
        bit = (h >> b) & 1
        source = term.at[c, :, :, 1 - bit] if b == 0 else landed[b - 1].at[c, :, 1 - bit]
        return pltpu.make_async_remote_copy(
            src_ref=source,
            dst_ref=landed[b].at[c],
            send_sem=s5.at[b, c],
            recv_sem=r5.at[b, c],
            device_id={"head": h + (1 - 2 * bit) * (1 << b)},
            device_id_type=MESH,
        )

    per_seq = p.ns // p.parts
    rows = []
    for part in range(p.parts):
        picks = [
            att[2 * (g // 3) + part, 2] if g % 3 == 1 else att[2 * (g // 3) + g % 3 // 2, part]
            for g in range(p.group)
        ]
        rows.append(jnp.concatenate(picks, axis=1))
    for c in range(p.chunks):
        cols = pl.ds(c * p.chunk, p.chunk)
        for part in range(p.parts):
            product = jnp.dot(rows[part], weight[:, cols], preferred_element_type=jnp.float32)
            term[c, pl.ds(part * per_seq, per_seq)] = product.astype(jnp.bfloat16).reshape(
                (per_seq,) + term.shape[2:]
            )
        halving(c, 0).start()

    def add_up(c, b):
        bit = (h >> b) & 1
        mine = term[c, :, :, bit] if b == 0 else landed[b - 1][c, :, bit]
        total = mine.astype(jnp.float32) + landed[b][c].astype(jnp.float32)
        landed[b][c] = total.astype(jnp.bfloat16)

    for b in range(p.bits - 1):
        for c in range(p.chunks):
            halving(c, b).wait_recv()
            add_up(c, b)
            halving(c, b + 1).start()
    summed = landed[p.bits - 1]

    def to_owner(c, ds, slot):
        to_s = lax.rem(s + ds, p.ns)
        return pltpu.make_async_remote_copy(
            src_ref=summed.at[c, to_s],
            dst_ref=final.at[c, slot],
            send_sem=s6.at[ds - 1, c],
            recv_sem=r6.at[ds - 1, c],
            device_id={"seq": to_s},
            device_id_type=MESH,
        )

    for c in range(p.chunks):
        halving(c, p.bits - 1).wait_recv()
        add_up(c, p.bits - 1)
        for ds in range(1, p.ns):
            to_owner(c, ds, s).start()
        final[c, s] = summed[c, s]
    for copy in late[1:]:
        copy.wait()

    sums = jnp.zeros((p.tokens, 1), jnp.float32)
    for c in range(p.chunks):
        for ds in range(1, p.ns):
            to_owner(c, ds, lax.rem(s - ds + p.ns, p.ns)).wait_recv()
        for j in range(p.ns):
            cols = pl.ds(j * p.columns + c * p.chunk, p.chunk)
            added = gate_ref[:, cols] * final[c, j].astype(jnp.float32)
            value = (res[:, cols].astype(jnp.float32) + added).astype(jnp.bfloat16)
            hidden_ref[:, cols] = value
            sums = sums + jnp.sum(value.astype(jnp.float32), -1, keepdims=True)
    mean = sums / p.width
    center = hidden_ref[...].astype(jnp.float32) - mean
    spread = jnp.mean(center * center, -1, keepdims=True)
    normed = center * lax.rsqrt(spread + 1e-06) * (1.0 + scale_ref[...]) + shift_ref[...]
    values = lax.dot_general(
        normed.astype(jnp.bfloat16),
        head_w[...],
        (((1,), (1,)), ((), ())),
        preferred_element_type=jnp.float32,
    )
    values = (values + bias_ref[...]).astype(jnp.bfloat16)
    features = values.shape[-1]
    patch[...] = jnp.zeros_like(patch)
    patch[:, :features] = values

    moves = [(0, 1), (0, -1), (1, 0), (1, 1), (1, -1)]

    def edge(index, sign):
        dh, ds = moves[index]
        return (
            (h + sign * dh >= 0) & (h + sign * dh < p.nh)
            & (s + sign * ds >= 0) & (s + sign * ds < p.ns)
        )

    def hop(index):
        dh, ds = moves[index]
        return pltpu.make_async_remote_copy(
            src_ref=patch,
            dst_ref=halo.at[index],
            send_sem=s7.at[index],
            recv_sem=r7.at[index],
            device_id={"seq": lax.rem(s + ds + p.ns, p.ns), "head": lax.rem(h + dh, p.nh)},
            device_id_type=MESH,
        )

    for index in range(len(moves)):

        @pl.when(edge(index, 1))
        def _():
            hop(index).start()

    near_ref[1, 1] = values
    for index, (dh, ds) in enumerate(moves):

        @pl.when(edge(index, -1))
        def _():
            hop(index).wait_recv()
            near_ref[1 - dh, 1 - ds] = halo[index][:, :features]

        @pl.when(jnp.logical_not(edge(index, -1)))
        def _():
            near_ref[1 - dh, 1 - ds] = jnp.zeros_like(values)

    for index in range(len(moves)):

        @pl.when(edge(index, 1))
        def _():
            hop(index).wait_send()

    for k in range(2):
        for index, (ds, dh) in enumerate(offsets):
            to_s, copy = sending(index, k)
            guarded(k, ds, s, to_s, copy.wait_send)
    for ds in range(1, p.ns):
        level = lax.rem(s - ds + p.ns, p.ns)

        @pl.when(handed(level))
        def _():
            hand_on(level, place(s, 0), place(peer_s, 0)).wait_send()

    for distance in range(p.ns):
        for i in range(p.units):

            @pl.when((s - distance >= 0) & up_open)
            def _():
                gather_hop(s - distance, i, 1).wait_send()

            @pl.when((s + distance < p.ns) & down_open)
            def _():
                gather_hop(s + distance, i, -1).wait_send()

    for c in range(p.chunks):
        for b in range(p.bits):
            halving(c, b).wait_send()
        for ds in range(1, p.ns):
            to_owner(c, ds, s).wait_send()


def on_device(
    queries,
    attn_keys,
    attn_values,
    residual,
    out_weight,
    out_gate,
    head_shift,
    head_scale,
    head_weight,
    head_bias,
    conv_weight,
    conv_bias,
    norm_gain,
):
    ns, nh = lax.axis_size("seq"), lax.axis_size("head")
    p = Plan(ns, nh, queries, residual, out_weight)
    if not p.fits(queries):
        return on_device_gathered(
            queries, attn_keys, attn_values, residual, out_weight, out_gate, head_shift,
            head_scale, head_weight, head_bias, conv_weight, conv_bias, norm_gain,
        )
    frames, height, breadth, inner = queries.shape
    t, width, patch_size = p.tokens, p.width, head_weight.shape[1]
    dma, bf16 = pltpu.SemaphoreType.DMA, jnp.bfloat16
    tail = (t, p.chunk)
    lanes = -(-patch_size // 128) * 128
    any_spec = pl.BlockSpec(memory_space=pl.ANY)
    vmem = pl.BlockSpec(memory_space=pltpu.VMEM)
    landed = [
        pltpu.VMEM((p.chunks, ns) + ((nh >> 1,) if b == 0 and nh > 2 else ()) + tail, bf16)
        for b in range(p.bits)
    ]
    hidden, near = pl.pallas_call(
        functools.partial(block_kernel, p),
        out_shape=(
            jax.ShapeDtypeStruct((t, width), bf16),
            jax.ShapeDtypeStruct((2, 3, t, patch_size), bf16),
        ),
        in_specs=[any_spec] * 6 + [vmem] * 4,
        out_specs=(vmem, vmem),
        scratch_shapes=[
            pltpu.VMEM((3, t, inner), bf16),
            pltpu.VMEM((p.slots, 2, 3, t, HEAD_DIM), bf16),
            pltpu.VMEM((ns, p.units, p.slots // p.parts * t, HEAD_DIM), bf16),
            pltpu.VMEM(out_weight.shape, bf16),
            pltpu.VMEM((t, width), bf16),
            pltpu.VMEM(head_weight.shape[::-1], bf16),
            pltpu.VMEM((p.chunks, ns, nh >> 1, 2) + tail, bf16),
            *landed,
            pltpu.VMEM((p.chunks, ns) + tail, bf16),
            pltpu.VMEM((t, lanes), bf16),
            pltpu.VMEM((5, t, lanes), bf16),
            dma((6,)),
            dma((2,)),
            dma((p.slots - 1, 2)),
            dma((p.slots - 1, 2)),
            dma((ns,)),
            dma((ns,)),
            dma((2, ns, p.units)),
            dma((ns, p.units)),
            dma((p.bits, p.chunks)),
            dma((p.bits, p.chunks)),
            dma((ns - 1, p.chunks)),
            dma((ns - 1, p.chunks)),
            dma((5,)),
            dma((5,)),
        ],
        compiler_params=pltpu.CompilerParams(
            collective_id=0, has_side_effects=True, vmem_limit_bytes=60 * 1024 * 1024
        ),
    )(
        queries.reshape(t, inner),
        attn_keys.reshape(t, inner),
        attn_values.reshape(t, inner),
        residual.reshape(t, width),
        out_weight,
        head_weight.T,
        out_gate.reshape(1, -1),
        head_shift.reshape(1, -1),
        head_scale.reshape(1, -1),
        head_bias.reshape(1, -1),
    )
    channels = patch_size // 4
    video = near.reshape(2, 3, frames, height, breadth, 2, 2, channels)
    video = video.transpose(0, 2, 1, 3, 5, 4, 6, 7)
    video = video.reshape(2, frames, 3 * height * 2, breadth * 2, channels)
    video = jnp.concatenate([video[0, -2:], video[1]], 0)
    rows = height * 2
    video = video[:, rows - 1 : 2 * rows + 1]
    padded = jnp.pad(video, ((0, 0), (0, 0), (1, 1), (0, 0)))
    features = convolve(padded, frames, conv_weight, conv_bias, norm_gain)
    return (hidden.reshape(residual.shape), features)


def solution(mesh):
    return jax.shard_map(
        on_device,
        mesh=mesh,
        in_specs=(
            P(("clip", "head"), "seq", None, None),
            P(("clip", "head"), "seq", None, None),
            P(("clip", "head"), "seq", None, None),
            P(("clip", "head"), "seq", None, None),
            P("head", "seq"),
            P(),
            P(),
            P(),
            P(),
            P(),
            P(),
            P(),
            P(),
        ),
        out_specs=(P(("clip", "head"), "seq", None, None), P(("clip", "head"), "seq", None, None)),
        check_vma=False,
    )
```

profile of v0, /device:TPU:0, one launch (start us, length us, event | category | flops | bytes accessed | tf_op | source)
XLA Modules:
  0.0 60.4 jit_solution(7078370284887533994)
XLA Ops:
  0.6 0.0 copy-start
  0.6 1.0 %copy-done = bf16[3,3,3,16,384]{4,3,2,1,0:T(8,128)(2,1)S(1)} copy-done((bf16[3,3,3,16,384]{4,3,2,1,0:T(8,128)(2,1)S(1)}, bf16[3,3,3,16,384]{4,3,2,1,0:T(8,128)(2,1)}, u32[]{:S(2)}) %copy-start) | copy-done | bytes 331800
  1.6 55.1 %shard_map.140 = (bf16[32,5120]{1,0:T(8,128)(2,1)}, bf16[2,3,32,64]{3,2,1,0:T(8,128)(2,1)}) custom-call(bf16[32,3072]{1,0:T(8,128)(2,1)} %bitcast.34, bf16[32,3072]{1,0:T(8,128)(2,1)} %bitcast.35, bf16[32,3072]{1,0:T(8,128)(2,1)} %bitcast.36, bf16[32,5120]{1,0:T(8,128)(2,1)} %bitcast.32, bf16[768,1280]{1,0:T(8,128)(2,1)} %w_hbm.1, ...), custom_call_target="tpu_custom_call" | custom-call | tf_op jit(solution)/shard_map/pallas_call | solution.py:586
  56.7 0.0 copy-start.2
  56.7 0.9 %reshape.67 = bf16[2,3,2,1,16,2,2,16]{7,6,5,4,2,1,0,3:T(2,128)(2,1)S(1)} reshape(bf16[2,3,32,64]{3,2,1,0:T(8,128)(2,1)} %get-tuple-element.5) | data formatting | bytes 49152 | tf_op jit(solution)/shard_map/reshape | solution.py:637
  57.6 0.2 copy.19
  57.8 0.0 copy-start.3
  57.8 0.2 fusion.3
  58.0 0.0 copy-start.1
  58.1 0.1 pad_slice_fusion.6
  58.2 0.3 concatenate.7
  58.6 0.0 copy-done.2
  58.6 0.3 multiply_reduce_fusion
  58.9 0.0 copy-done.3
  58.9 0.8 %multiply_convert_fusion = bf16[128,384]{1,0:T(8,128)(2,1)} fusion(f32[128,384]{1,0:T(8,128)S(1)} %get-tuple-element.40, f32[384]{0:T(512)S(1)} %copy-done.3, f32[128]{0:T(128)S(1)} %add_rsqrt_fusion), kind=kLoop, calls=%fused_computation.8 | loop fusion | flops 344064 | bytes 296960 | tf_op jit(solution)/shard_map/convert_element_type | solution.py:72
  59.7 0.0 copy-done.1
  59.7 0.7 %copy.21 = bf16[2,1,16,5120]{3,2,1,0:T(8,128)(2,1)} copy(bf16[2,1,16,5120]{3,2,1,0:T(8,128)(2,1)S(1)} %bitcast.33) | data formatting | bytes 655360
  (3 shorter events, 0.1 us)
Async XLA Ops:
  0.6 1.0 %copy-start = (bf16[3,3,3,16,384]{4,3,2,1,0:T(8,128)(2,1)S(1)}, bf16[3,3,3,16,384]{4,3,2,1,0:T(8,128)(2,1)}, u32[]{:S(2)}) copy-start(bf16[3,3,3,16,384]{4,3,2,1,0:T(8,128)(2,1)} %param.23) | copy-start | bytes 995332
  56.7 1.9 %copy-start.2 = (f32[384]{0:T(512)S(1)}, f32[384]{0:T(512)}, u32[]{:S(2)}) copy-start(f32[384]{0:T(512)} %param.24) | copy-start | bytes 4612
  57.8 1.1 %copy-start.3 = (f32[384]{0:T(512)S(1)}, f32[384]{0:T(512)}, u32[]{:S(2)}) copy-start(f32[384]{0:T(512)} %param.25) | copy-start | bytes 4612
  58.0 1.7 %copy-start.1 = (bf16[32,5120]{1,0:T(8,128)(2,1)S(1)}, bf16[32,5120]{1,0:T(8,128)(2,1)}, u32[]{:S(2)}) copy-start(bf16[32,5120]{1,0:T(8,128)(2,1)} %get-tuple-element.4) | copy-start | bytes 983044
where the time goes:
time: 60.7 us; the launch traced here: 60.4 us
  Pallas kernels  55.1 us (91%)
  local copies, waits for them, and re-layouts  3.45 us (6%)
  other arithmetic  0.84 us (1%)
  between operations  0.75 us (1%)
    pallas_call x1, Pallas kernels, on_device(): pl.pallas_call(functools.partial(block_kernel, p), out_shape=(jax.ShapeDt...  55.1 us
    unnamed x9, local copies, waits for them, and re-layouts  1.71 us

commit v1 on v0

v1 whole, which is shorter than its diff:
```python
import functools
import math

import jax
import jax.numpy as jnp
from jax import lax
from jax.experimental import pallas as pl
from jax.experimental.pallas import tpu as pltpu
from jax.sharding import PartitionSpec as P

HEAD_DIM = 128


def from_behind(value, axis, steps):
    count = lax.axis_size(axis)
    first, last = (max(0, -steps), min(count, count - steps))
    return lax.ppermute(value, axis, [(source, source + steps) for source in range(first, last)])


def padded_2(x, sides, width):
    for axis, dim in sides:
        peers, length = (lax.axis_size(axis), x.shape[dim])
        up = [(i, (i + 1) % peers) for i in range(peers - 1)]
        down = [(j, i) for i, j in up]
        last = lax.slice_in_dim(x, length - width, length, axis=dim)
        first = lax.slice_in_dim(x, 0, width, axis=dim)
        before = lax.ppermute(last, axis, up)
        after = lax.ppermute(first, axis, down)
        x = jnp.concatenate([before, x, after], axis=dim)
    return x


def head_latent(hidden, head_shift, head_scale, head_weight, head_bias):
    values = hidden.astype(jnp.float32)
    center = values - jnp.mean(values, -1, keepdims=True)
    spread = jnp.mean(center * center, -1, keepdims=True)
    normed = (center * lax.rsqrt(spread + 1e-06) * (1.0 + head_scale) + head_shift).astype(
        jnp.bfloat16
    )
    flat = normed.reshape(-1, normed.shape[-1])
    latent = (jnp.dot(flat, head_weight, preferred_element_type=jnp.float32) + head_bias).astype(
        jnp.bfloat16
    )
    frames, height, breadth = (hidden.shape[0], hidden.shape[1], hidden.shape[2])
    channels = head_weight.shape[1] // 4
    patches = latent.reshape(frames, height, breadth, 2, 2, channels).transpose(0, 1, 3, 2, 4, 5)
    return patches.reshape(frames, height * 2, breadth * 2, channels)


def convolve(padded, frames, conv_weight, conv_bias, norm_gain):
    height = padded.shape[1] - 2
    breadth = padded.shape[2] - 2
    stacked = jnp.concatenate(
        [
            padded[
                time_off : time_off + frames,
                row_off : row_off + height,
                col_off : col_off + breadth,
            ]
            for time_off in range(3)
            for row_off in range(3)
            for col_off in range(3)
        ],
        -1,
    )
    kernel = conv_weight.reshape(-1, conv_weight.shape[-1])
    linear = (
        jnp.dot(stacked.reshape(-1, stacked.shape[-1]), kernel, preferred_element_type=jnp.float32)
        + conv_bias
    )
    normed = linear * lax.rsqrt(jnp.mean(linear * linear, -1, keepdims=True) + 1e-06) * norm_gain
    return jax.nn.silu(normed).astype(jnp.bfloat16).reshape(frames, height, breadth, -1)


def attend_block(carried, block_keys, block_values, query_heads):
    running, denominator, weighted = carried
    scores = jnp.einsum("hqd,khd->hqk", query_heads, block_keys, preferred_element_type=jnp.float32)
    scores = scores * query_heads.shape[-1] ** (-0.5)
    newmax = jnp.maximum(running, jnp.max(scores, -1))
    factor = jnp.exp(running - newmax)
    weights = jnp.exp(scores - newmax[..., None])
    denominator = denominator * factor + jnp.sum(weights, -1)
    product = jnp.einsum(
        "hqk,khd->hqd",
        weights.astype(jnp.bfloat16),
        block_values,
        preferred_element_type=jnp.float32,
    )
    weighted = weighted * factor[..., None] + product
    return (newmax, denominator, weighted)


def fold_pieces(query_heads, carried, pieces):
    key_piece, value_piece = pieces
    frames, height, breadth = (key_piece.shape[0], key_piece.shape[1], key_piece.shape[2])
    heads_here, head_width = (query_heads.shape[0], query_heads.shape[2])
    group_rows = 4

    def regroup(one_piece):
        shaped = one_piece.reshape(
            frames, height // group_rows, group_rows, breadth, heads_here, head_width
        )
        shaped = shaped.transpose(1, 0, 2, 3, 4, 5)
        return shaped.reshape(
            height // group_rows, frames * group_rows * breadth, heads_here, head_width
        )

    def advance(inner, blocks):
        return (attend_block(inner, blocks[0], blocks[1], query_heads), None)

    carried, _ = lax.scan(advance, carried, (regroup(key_piece), regroup(value_piece)))
    return carried


def on_device_gathered(
    queries,
    attn_keys,
    attn_values,
    residual,
    out_weight,
    out_gate,
    head_shift,
    head_scale,
    head_weight,
    head_bias,
    conv_weight,
    conv_bias,
    norm_gain,
):
    head_count = lax.axis_size("head")
    frames_dev = queries.shape[0]
    group_width = queries.shape[3] // head_count
    head_width = HEAD_DIM
    heads_here = group_width // head_width
    local_queries, local_keys, local_values = (
        lax.all_to_all(queries, "head", split_axis=3, concat_axis=0, tiled=True),
        lax.all_to_all(attn_keys, "head", split_axis=3, concat_axis=0, tiled=True),
        lax.all_to_all(attn_values, "head", split_axis=3, concat_axis=0, tiled=True),
    )
    frames_all, height, breadth = (
        local_queries.shape[0],
        local_queries.shape[1],
        local_queries.shape[2],
    )
    count = frames_all * height * breadth
    query_heads = local_queries.reshape(count, heads_here, head_width).transpose(1, 0, 2)
    initial = (
        jnp.full((heads_here, count), -1e30, jnp.float32),
        jnp.zeros((heads_here, count), jnp.float32),
        jnp.zeros((heads_here, count, head_width), jnp.float32),
    )
    carried = fold_pieces(
        query_heads,
        initial,
        (
            lax.all_gather(local_keys, "seq", axis=1, tiled=True),
            lax.all_gather(local_values, "seq", axis=1, tiled=True),
        ),
    )
    running, denominator, weighted = carried
    attended = (weighted / denominator[..., None]).astype(jnp.bfloat16)
    attended = attended.transpose(1, 0, 2).reshape(count, group_width)
    partial_value = jnp.dot(
        attended,
        lax.all_gather(out_weight, "seq", axis=1, tiled=True),
        preferred_element_type=jnp.float32,
    )
    partial_value = partial_value.reshape(frames_all, height, breadth, partial_value.shape[-1])
    owned = lax.psum_scatter(
        partial_value.astype(jnp.bfloat16), "head", scatter_dimension=0, tiled=True
    ).astype(jnp.float32)
    hidden = (residual.astype(jnp.float32) + out_gate * owned).astype(jnp.bfloat16)
    own_video = head_latent(hidden, head_shift, head_scale, head_weight, head_bias)
    earlier = from_behind(own_video, "head", 1)
    video = jnp.concatenate([earlier, own_video], 0)
    extended = padded_2(video, (("seq", 1),), 1)
    padded = jnp.pad(extended, ((0, 0), (0, 0), (1, 1), (0, 0)))
    features = convolve(padded, frames_dev, conv_weight, conv_bias, norm_gain)
    return (hidden, features)


MESH = pl.DeviceIdType.MESH


class Plan:
    def __init__(self, ns, nh, queries, residual, out_weight):
        self.ns, self.nh = ns, nh
        self.frames = queries.shape[0]
        self.cells = queries.shape[1] * queries.shape[2]
        self.inner = queries.shape[3]
        self.tokens = self.frames * self.cells
        self.group = self.inner // nh // HEAD_DIM
        self.few = max(1, self.group // 6)
        self.width = residual.shape[3]
        self.columns = out_weight.shape[1]
        self.slots = ns * nh
        self.chunk = 256 if self.columns % 256 == 0 else 128
        self.chunks = self.columns // self.chunk
        self.counts = (2 * self.few, self.few, self.few, 2 * self.few)
        self.owner = [o for o, count in enumerate(self.counts) for _ in range(count)]

    def fits(self, queries):
        return (
            self.nh == 4
            and self.ns == 4
            and self.group == 6 * self.few
            and self.inner == self.nh * self.group * HEAD_DIM
            and self.frames == 2
            and self.cells % 16 == 0
            and self.columns % 128 == 0
            and self.slots * self.tokens <= 1024
        )


SENDS = ((2, 1), (2, 0), (1, 3), (1, 2))
RELAY = ((2, 3), (2, 3), (1, 0), (1, 0))


def block_kernel(
    plan,
    q_hbm, k_hbm, v_hbm, res_hbm, w_hbm, hw_hbm,
    gate_ref, shift_ref, scale_ref, bias_ref,
    hidden_ref, near_ref,
    qkv, qs, kv, att, weight, res, head_w, term, landed0, landed1, final, patch, halo,
    local_sem, s1, r1, s3, r3, s5, r5, s6, r6, s7, r7,
):
    p = plan
    s = lax.axis_index("seq")
    h = lax.axis_index("head")
    core, across = h & 1, h >> 1

    def slot(seq_index, head_index):
        return ((head_index & 1) * 2 + (head_index >> 1)) * p.ns + seq_index

    here = slot(s, h)
    at_end = (s == 0) | (s == p.ns - 1)
    offsets = [(ds, dh) for ds in (2, 1, 3, 0) for dh in range(p.nh) if ds or dh]
    widths = ((2 * p.few, True), (p.few, False))

    def columns_of(seq_index, head_index):
        before = p.few * (seq_index + jnp.minimum(seq_index, 1))
        return pl.multiple_of((head_index * p.group + before) * HEAD_DIM, HEAD_DIM)

    loads = [
        pltpu.make_async_copy(q_hbm, qkv.at[0], local_sem.at[0]),
        pltpu.make_async_copy(k_hbm, qkv.at[1], local_sem.at[1]),
        pltpu.make_async_copy(v_hbm, qkv.at[2], local_sem.at[2]),
    ]
    late = [
        pltpu.make_async_copy(w_hbm, weight, local_sem.at[3]),
        pltpu.make_async_copy(res_hbm, res, local_sem.at[4]),
        pltpu.make_async_copy(hw_hbm, head_w, local_sem.at[5]),
    ]

    def own_copies(heads):
        cols, fill = pl.ds(columns_of(s, h), heads * HEAD_DIM), pl.ds(0, heads * HEAD_DIM)
        return [
            pltpu.make_async_copy(q_hbm.at[:, :, cols], qs.at[:, here, :, fill], local_sem.at[6]),
            pltpu.make_async_copy(k_hbm.at[:, :, cols], kv.at[0, :, here, :, fill], local_sem.at[7]),
            pltpu.make_async_copy(v_hbm.at[:, :, cols], kv.at[1, :, here, :, fill], local_sem.at[8]),
        ]

    def by_class(end, act):
        for heads, wanted in widths:
            pl.when(end == wanted)(functools.partial(act, heads))

    for copy in loads:
        copy.start()

    barrier = pltpu.get_barrier_semaphore()
    for ds, dh in offsets:
        pl.semaphore_signal(
            barrier,
            inc=1,
            device_id={"seq": lax.rem(s + ds, p.ns), "head": lax.rem(h + dh, p.nh)},
            device_id_type=MESH,
        )

    @functools.partial(by_class, at_end)
    def _(heads):
        for copy in own_copies(heads):
            copy.start()

    for copy in loads:
        copy.wait()
    pl.semaphore_wait(barrier, len(offsets))

    def exchange(phase, index, from_slot, to_s, to_h, heads):
        cols, fill = pl.ds(columns_of(to_s, to_h), heads * HEAD_DIM), pl.ds(0, heads * HEAD_DIM)
        if phase == 0:
            source, target = qkv.at[pl.ds(1, 2), :, :, cols], kv.at[:, :, from_slot, :, fill]
        else:
            source, target = qkv.at[0, phase - 1, :, cols], qs.at[phase - 1, from_slot, :, fill]
        return pltpu.make_async_remote_copy(
            src_ref=source,
            dst_ref=target,
            send_sem=s1.at[phase, index],
            recv_sem=r1.at[phase, index],
            device_id={"seq": to_s, "head": to_h},
            device_id_type=MESH,
        )

    def for_sends(phase, act):
        for ds in sorted(set(ds for ds, _ in offsets), key=[2, 1, 3, 0].index):
            to_s = lax.rem(s + ds, p.ns)

            @functools.partial(by_class, (to_s == 0) | (to_s == p.ns - 1))
            def _(heads, ds=ds, to_s=to_s):
                for index, (ds2, dh) in enumerate(offsets):
                    if ds2 == ds:
                        act(exchange(phase, index, here, to_s, lax.rem(h + dh, p.nh), heads))

    def arrivals(phase):
        @functools.partial(by_class, at_end)
        def _(heads):
            for index, (ds, dh) in enumerate(offsets):
                from_s, from_h = lax.rem(s - ds + p.ns, p.ns), lax.rem(h - dh + p.nh, p.nh)
                exchange(phase, index, slot(from_s, from_h), s, h, heads).wait_recv()

    for phase in range(3):
        for_sends(phase, lambda copy: copy.start())
    for copy in late:
        copy.start()

    def hop(head, f, to_s, way):
        return pltpu.make_async_remote_copy(
            src_ref=att.at[f, head],
            dst_ref=att.at[f, head],
            send_sem=s3.at[way, f, head],
            recv_sem=r3.at[f, head],
            device_id={"seq": to_s},
            device_id_type=MESH,
        )

    def attend(f, j):
        lanes = slice(j * HEAD_DIM, (j + 1) * HEAD_DIM)
        q = qs[f, :, :, lanes].reshape(-1, HEAD_DIM)
        k = kv[0, :, :, :, lanes].reshape(-1, HEAD_DIM)
        v = kv[1, :, :, :, lanes].reshape(-1, HEAD_DIM)
        scores = lax.dot_general(
            q, k, (((1,), (1,)), ((), ())), preferred_element_type=jnp.float32
        )
        scores = scores * HEAD_DIM ** (-0.5)
        weights = jnp.exp(scores - jnp.max(scores, -1, keepdims=True))
        denominator = jnp.sum(weights, -1, keepdims=True)
        product = jnp.dot(weights.astype(jnp.bfloat16), v, preferred_element_type=jnp.float32)
        att[f, p.few * (s + jnp.minimum(s, 1)) + j] = (product / denominator).astype(jnp.bfloat16)

    def send_own(f, j, way):
        for o in range(p.ns):
            if j < p.counts[o]:
                head = p.owner.index(o) + j

                @pl.when(s == o)
                def _():
                    hop(head, f, SENDS[o][way], way).start()

    for f in range(p.frames):
        if f == 0:
            @functools.partial(by_class, at_end)
            def _(heads):
                for copy in own_copies(heads):
                    copy.wait()

            arrivals(0)
        arrivals(1 + f)
        for j in range(p.few):
            attend(f, j)
            send_own(f, j, 0)
        for j in range(p.few, 2 * p.few):
            @pl.when(at_end)
            def _():
                attend(f, j)

            send_own(f, j, 0)
        for j in range(2 * p.few):
            send_own(f, j, 1)

    def order(row):
        others = [head for head in range(p.group) if p.owner[head] != row]
        relayed = {head: row == RELAY[p.owner[head]][0] for head in others}
        return sorted(
            others,
            key=lambda head: (
                abs(p.owner[head] - row) if relayed[head] or row in (0, p.ns - 1) else 9, head,
            ),
        )

    def take(f, head, row):
        hop(head, f, row, 0).wait_recv()
        relay, last = RELAY[p.owner[head]]
        if row == relay:
            hop(head, f, last, 0).start()

    def gather(todo):
        for row in range(p.ns):
            @pl.when(s == row)
            def _():
                for f, head in todo(row):
                    take(f, head, row)

    def first_part(row):
        heads = order(row)
        near = [head for head in heads if abs(p.owner[head] - row) == 1 and p.owner[head] in (1, 2)]
        early = near if row in (1, 2) else []
        return [(0, head) for head in early] + [(1, head) for head in early] + [
            (0, head) for head in heads if head not in early
        ]

    def second_part(row):
        done = first_part(row)
        return [(1, head) for head in order(row) if (1, head) not in done]

    def halving(f, c, b):
        bit = core if b == 0 else across
        source = term.at[f, c, 1 - bit] if b == 0 else landed0.at[f, c, 1 - bit]
        target = landed0.at[f, c] if b == 0 else landed1.at[f, c]
        return pltpu.make_async_remote_copy(
            src_ref=source,
            dst_ref=target,
            send_sem=s5.at[b, f, c],
            recv_sem=r5.at[b, f, c],
            device_id={"head": h + (1 - 2 * bit) * (1 << b)},
            device_id_type=MESH,
        )

    def project(f, c):
        cols = pl.ds(c * p.chunk, p.chunk)
        rows = jnp.concatenate([att[f, head] for head in range(p.group)], axis=1)
        product = jnp.dot(rows, weight[:, cols], preferred_element_type=jnp.float32)
        term[f, c] = product.astype(jnp.bfloat16).reshape(term.shape[2:])
        halving(f, c, 0).start()

    def pair_sum(f, c):
        halving(f, c, 0).wait_recv()
        total = term[f, c, core].astype(jnp.float32) + landed0[f, c].astype(jnp.float32)
        landed0[f, c] = total.astype(jnp.bfloat16)
        halving(f, c, 1).start()

    def to_owner(f, c, ds, row):
        to_s = lax.rem(s + ds, p.ns)
        return pltpu.make_async_remote_copy(
            src_ref=landed1.at[f, c, to_s],
            dst_ref=final.at[f, c, row],
            send_sem=s6.at[ds - 1, f, c],
            recv_sem=r6.at[ds - 1, f, c],
            device_id={"seq": to_s},
            device_id_type=MESH,
        )

    def full_sum(f, c):
        halving(f, c, 1).wait_recv()
        total = landed0[f, c, across].astype(jnp.float32) + landed1[f, c].astype(jnp.float32)
        landed1[f, c] = total.astype(jnp.bfloat16)
        for ds in (2, 1, 3):
            to_owner(f, c, ds, s).start()
        final[f, c, s] = landed1[f, c, s]

    gather(first_part)
    late[0].wait()
    for c in range(p.chunks):
        project(0, c)
    for c in range(p.chunks):
        pair_sum(0, c)
    gather(second_part)
    for c in range(p.chunks):
        project(1, c)
    for c in range(p.chunks):
        pair_sum(1, c)
        full_sum(0, c)
    for copy in late[1:]:
        copy.wait()

    def finish(f, c, sums):
        for ds in range(1, p.ns):
            to_owner(f, c, ds, lax.rem(s - ds + p.ns, p.ns)).wait_recv()
        rows = slice(f * p.cells, (f + 1) * p.cells)
        for j in range(p.ns):
            cols = slice(j * p.columns + c * p.chunk, j * p.columns + (c + 1) * p.chunk)
            added = gate_ref[:, cols] * final[f, c, j].astype(jnp.float32)
            value = (res[rows, cols].astype(jnp.float32) + added).astype(jnp.bfloat16)
            hidden_ref[rows, cols] = value
            sums = sums + jnp.sum(value.astype(jnp.float32), -1, keepdims=True)
        return sums

    sums = [jnp.zeros((p.cells, 1), jnp.float32) for _ in range(p.frames)]
    for c in range(p.chunks):
        full_sum(1, c)
        sums[0] = finish(0, c, sums[0])
    for c in range(p.chunks):
        sums[1] = finish(1, c, sums[1])
    mean = jnp.concatenate(sums, axis=0) / p.width
    center = hidden_ref[...].astype(jnp.float32) - mean
    spread = jnp.mean(center * center, -1, keepdims=True)
    normed = center * lax.rsqrt(spread + 1e-06) * (1.0 + scale_ref[...]) + shift_ref[...]
    values = lax.dot_general(
        normed.astype(jnp.bfloat16),
        head_w[...],
        (((1,), (1,)), ((), ())),
        preferred_element_type=jnp.float32,
    )
    values = (values + bias_ref[...]).astype(jnp.bfloat16)
    features = values.shape[-1]
    patch[...] = jnp.zeros_like(patch)
    patch[:, :features] = values

    moves = [(0, 1), (0, -1), (1, 0), (1, 1), (1, -1)]

    def edge(index, sign):
        dh, ds = moves[index]
        return (
            (h + sign * dh >= 0) & (h + sign * dh < p.nh)
            & (s + sign * ds >= 0) & (s + sign * ds < p.ns)
        )

    def reach(index):
        dh, ds = moves[index]
        return pltpu.make_async_remote_copy(
            src_ref=patch,
            dst_ref=halo.at[index],
            send_sem=s7.at[index],
            recv_sem=r7.at[index],
            device_id={"seq": lax.rem(s + ds + p.ns, p.ns), "head": lax.rem(h + dh, p.nh)},
            device_id_type=MESH,
        )

    for index in range(len(moves)):

        @pl.when(edge(index, 1))
        def _():
            reach(index).start()

    near_ref[1, 1] = values
    for index, (dh, ds) in enumerate(moves):

        @pl.when(edge(index, -1))
        def _():
            reach(index).wait_recv()
            near_ref[1 - dh, 1 - ds] = halo[index][:, :features]

        @pl.when(jnp.logical_not(edge(index, -1)))
        def _():
            near_ref[1 - dh, 1 - ds] = jnp.zeros_like(values)

    for index in range(len(moves)):

        @pl.when(edge(index, 1))
        def _():
            reach(index).wait_send()

    for phase in range(3):
        for_sends(phase, lambda copy: copy.wait_send())

    for row in range(p.ns):
        @pl.when(s == row)
        def _():
            for f in range(p.frames):
                for head in range(p.group):
                    o = p.owner[head]
                    if o == row:
                        for way in range(2):
                            hop(head, f, SENDS[o][way], way).wait_send()
                    elif RELAY[o][0] == row:
                        hop(head, f, RELAY[o][1], 0).wait_send()

    for f in range(p.frames):
        for c in range(p.chunks):
            for b in range(2):
                halving(f, c, b).wait_send()
            for ds in range(1, p.ns):
                to_owner(f, c, ds, s).wait_send()


def on_device(
    queries,
    attn_keys,
    attn_values,
    residual,
    out_weight,
    out_gate,
    head_shift,
    head_scale,
    head_weight,
    head_bias,
    conv_weight,
    conv_bias,
    norm_gain,
):
    ns, nh = lax.axis_size("seq"), lax.axis_size("head")
    p = Plan(ns, nh, queries, residual, out_weight)
    if not p.fits(queries):
        return on_device_gathered(
            queries, attn_keys, attn_values, residual, out_weight, out_gate, head_shift,
            head_scale, head_weight, head_bias, conv_weight, conv_bias, norm_gain,
        )
    frames, height, breadth, inner = queries.shape
    t, cells, width, patch_size = p.tokens, p.cells, p.width, head_weight.shape[1]
    dma, bf16 = pltpu.SemaphoreType.DMA, jnp.bfloat16
    lanes = -(-patch_size // 128) * 128
    most = 2 * p.few * HEAD_DIM
    any_spec = pl.BlockSpec(memory_space=pl.ANY)
    vmem = pl.BlockSpec(memory_space=pltpu.VMEM)
    hidden, near = pl.pallas_call(
        functools.partial(block_kernel, p),
        out_shape=(
            jax.ShapeDtypeStruct((t, width), bf16),
            jax.ShapeDtypeStruct((2, 3, t, patch_size), bf16),
        ),
        in_specs=[any_spec] * 6 + [vmem] * 4,
        out_specs=(vmem, vmem),
        scratch_shapes=[
            pltpu.VMEM((3, frames, cells, inner), bf16),
            pltpu.VMEM((frames, p.slots, cells, most), bf16),
            pltpu.VMEM((2, frames, p.slots, cells, most), bf16),
            pltpu.VMEM((frames, p.group, p.slots * cells, HEAD_DIM), bf16),
            pltpu.VMEM(out_weight.shape, bf16),
            pltpu.VMEM((t, width), bf16),
            pltpu.VMEM(head_weight.shape[::-1], bf16),
            pltpu.VMEM((frames, p.chunks, 2, 2, ns, cells, p.chunk), bf16),
            pltpu.VMEM((frames, p.chunks, 2, ns, cells, p.chunk), bf16),
            pltpu.VMEM((frames, p.chunks, ns, cells, p.chunk), bf16),
            pltpu.VMEM((frames, p.chunks, ns, cells, p.chunk), bf16),
            pltpu.VMEM((t, lanes), bf16),
            pltpu.VMEM((5, t, lanes), bf16),
            dma((9,)),
            dma((3, p.slots - 1)),
            dma((3, p.slots - 1)),
            dma((2, frames, p.group)),
            dma((frames, p.group)),
            dma((2, frames, p.chunks)),
            dma((2, frames, p.chunks)),
            dma((ns - 1, frames, p.chunks)),
            dma((ns - 1, frames, p.chunks)),
            dma((5,)),
            dma((5,)),
        ],
        compiler_params=pltpu.CompilerParams(
            collective_id=0, has_side_effects=True, vmem_limit_bytes=60 * 1024 * 1024
        ),
    )(
        queries.reshape(frames, cells, inner),
        attn_keys.reshape(frames, cells, inner),
        attn_values.reshape(frames, cells, inner),
        residual.reshape(t, width),
        out_weight,
        head_weight.T,
        out_gate.reshape(1, -1),
        head_shift.reshape(1, -1),
        head_scale.reshape(1, -1),
        head_bias.reshape(1, -1),
    )
    channels = patch_size // 4
    video = near.reshape(2, 3, frames, height, breadth, 2, 2, channels)
    video = video.transpose(0, 2, 1, 3, 5, 4, 6, 7)
    video = video.reshape(2, frames, 3 * height * 2, breadth * 2, channels)
    video = jnp.concatenate([video[0, -2:], video[1]], 0)
    rows = height * 2
    video = video[:, rows - 1 : 2 * rows + 1]
    padded = jnp.pad(video, ((0, 0), (0, 0), (1, 1), (0, 0)))
    features = convolve(padded, frames, conv_weight, conv_bias, norm_gain)
    return (hidden.reshape(residual.shape), features)


def solution(mesh):
    return jax.shard_map(
        on_device,
        mesh=mesh,
        in_specs=(
            P(("clip", "head"), "seq", None, None),
            P(("clip", "head"), "seq", None, None),
            P(("clip", "head"), "seq", None, None),
            P(("clip", "head"), "seq", None, None),
            P("head", "seq"),
            P(),
            P(),
            P(),
            P(),
            P(),
            P(),
            P(),
            P(),
        ),
        out_specs=(P(("clip", "head"), "seq", None, None), P(("clip", "head"), "seq", None, None)),
        check_vma=False,
    )
```

time: 60.7 us -> 62.1 us (1.023)
  Pallas kernels: 55.1 us -> 56.4 us
    pallas_call x1, Pallas kernels: 55.1 us -> 56.4 us  [on_device(): pl.pallas_call(functools.partial(block_kernel, p), out_shape=(jax.ShapeDt...]
where the time goes in v1:
time: 62.1 us; the launch traced here: 61.8 us
  Pallas kernels  56.4 us (91%)
  local copies, waits for them, and re-layouts  3.45 us (6%)
  other arithmetic  0.84 us (1%)
  between operations  0.75 us (1%)
    pallas_call x1, Pallas kernels, on_device(): pl.pallas_call(functools.partial(block_kernel, p), out_shape=(jax.ShapeDt...  56.4 us
    unnamed x9, local copies, waits for them, and re-layouts  1.71 us

profile of v1, /device:TPU:0, one launch (start us, length us, event | category | flops | bytes accessed | tf_op | source)
XLA Modules:
  0.0 61.8 jit_solution(10960706537901974711)
XLA Ops:
  0.6 0.0 copy-start
  0.6 1.0 %copy-done = bf16[3,3,3,16,384]{4,3,2,1,0:T(8,128)(2,1)S(1)} copy-done((bf16[3,3,3,16,384]{4,3,2,1,0:T(8,128)(2,1)S(1)}, bf16[3,3,3,16,384]{4,3,2,1,0:T(8,128)(2,1)}, u32[]{:S(2)}) %copy-start) | copy-done | bytes 331800
  1.6 56.4 %shard_map.140 = (bf16[32,5120]{1,0:T(8,128)(2,1)}, bf16[2,3,32,64]{3,2,1,0:T(8,128)(2,1)}) custom-call(bf16[2,16,3072]{2,1,0:T(8,128)(2,1)} %bitcast.34, bf16[2,16,3072]{2,1,0:T(8,128)(2,1)} %bitcast.35, bf16[2,16,3072]{2,1,0:T(8,128)(2,1)} %bitcast.36, bf16[32,5120]{1,0:T(8,128)(2,1)} %bitcast.32, bf16[768,1280]{1,0:T(8,128)(2,1)} %w_hbm.1, ...), custom_call_target="tpu_custom_call" | custom-call | tf_op jit(solution)/shard_map/pallas_call | solution.py:603
  58.1 0.0 copy-start.2
  58.1 0.9 %reshape.67 = bf16[2,3,2,1,16,2,2,16]{7,6,5,4,2,1,0,3:T(2,128)(2,1)S(1)} reshape(bf16[2,3,32,64]{3,2,1,0:T(8,128)(2,1)} %get-tuple-element.5) | data formatting | bytes 49152 | tf_op jit(solution)/shard_map/reshape | solution.py:653
  59.0 0.2 copy.19
  59.2 0.0 copy-start.3
  59.2 0.2 fusion.3
  59.4 0.0 copy-start.1
  59.4 0.1 pad_slice_fusion.6
  59.6 0.3 concatenate.7
  59.9 0.0 copy-done.2
  60.0 0.3 multiply_reduce_fusion
  60.3 0.0 copy-done.3
  60.3 0.8 %multiply_convert_fusion = bf16[128,384]{1,0:T(8,128)(2,1)} fusion(f32[128,384]{1,0:T(8,128)S(1)} %get-tuple-element.40, f32[384]{0:T(512)S(1)} %copy-done.3, f32[128]{0:T(128)S(1)} %add_rsqrt_fusion), kind=kLoop, calls=%fused_computation.8 | loop fusion | flops 344064 | bytes 296960 | tf_op jit(solution)/shard_map/convert_element_type | solution.py:72
  61.1 0.0 copy-done.1
  61.1 0.7 %copy.21 = bf16[2,1,16,5120]{3,2,1,0:T(8,128)(2,1)} copy(bf16[2,1,16,5120]{3,2,1,0:T(8,128)(2,1)S(1)} %bitcast.33) | data formatting | bytes 655360
  (3 shorter events, 0.1 us)
Async XLA Ops:
  0.6 1.0 %copy-start = (bf16[3,3,3,16,384]{4,3,2,1,0:T(8,128)(2,1)S(1)}, bf16[3,3,3,16,384]{4,3,2,1,0:T(8,128)(2,1)}, u32[]{:S(2)}) copy-start(bf16[3,3,3,16,384]{4,3,2,1,0:T(8,128)(2,1)} %param.23) | copy-start | bytes 995332
  58.1 1.9 %copy-start.2 = (f32[384]{0:T(512)S(1)}, f32[384]{0:T(512)}, u32[]{:S(2)}) copy-start(f32[384]{0:T(512)} %param.24) | copy-start | bytes 4612
  59.2 1.1 %copy-start.3 = (f32[384]{0:T(512)S(1)}, f32[384]{0:T(512)}, u32[]{:S(2)}) copy-start(f32[384]{0:T(512)} %param.25) | copy-start | bytes 4612
  59.4 1.7 %copy-start.1 = (bf16[32,5120]{1,0:T(8,128)(2,1)S(1)}, bf16[32,5120]{1,0:T(8,128)(2,1)}, u32[]{:S(2)}) copy-start(bf16[32,5120]{1,0:T(8,128)(2,1)} %get-tuple-element.4) | copy-start | bytes 983044

commit v2 on v1

--- a/solution.py
+++ b/solution.py
@@ -196,10 +196,11 @@
         self.slots = ns * nh
         self.chunk = 256 if self.columns % 256 == 0 else 128
         self.chunks = self.columns // self.chunk
+        self.cuts = 2
         self.counts = (2 * self.few, self.few, self.few, 2 * self.few)
         self.owner = [o for o, count in enumerate(self.counts) for _ in range(count)]
 
-    def fits(self, queries):
+    def fits(self, queries, head_weight, conv_weight):
         return (
             self.nh == 4
             and self.ns == 4
@@ -208,26 +209,43 @@
             and self.frames == 2
             and self.cells % 16 == 0
             and self.columns % 128 == 0
+            and queries.shape[1] == 1
+            and head_weight.shape[1] == 64
+            and conv_weight.shape[3] == 16
+            and conv_weight.shape[4] % 128 == 0
             and self.slots * self.tokens <= 1024
         )
 
 
-SENDS = ((2, 1), (2, 0), (1, 3), (1, 2))
-RELAY = ((2, 3), (2, 3), (1, 0), (1, 0))
+def source_row(o, j, row):
+    step = 1 if row > o else -1
+    if o in (1, 2) or j % 2 == 0:
+        return row - step
+    return o if abs(row - o) < 3 else row - step
+
+
+def due(o, j, f, row):
+    away = abs(row - o)
+    if o in (1, 2):
+        return 3.0 * away
+    if j % 2 == 0:
+        return 14.4 + 2.8 * f + 2.8 * away
+    return 20.4 + 1.4 * f + 2.4 if away == 1 else 16.7 + 2.8 * f + 2.8 * (away - 1)
 
 
 def block_kernel(
     plan,
     q_hbm, k_hbm, v_hbm, res_hbm, w_hbm, hw_hbm,
-    gate_ref, shift_ref, scale_ref, bias_ref,
-    hidden_ref, near_ref,
-    qkv, qs, kv, att, weight, res, head_w, term, landed0, landed1, final, patch, halo,
+    gate_hbm, shift_hbm, scale_hbm, bias_hbm, cw_hbm, cb_hbm, gain_hbm,
+    hidden_ref, near_ref, wide_ref, rows_ref,
+    qkv, got, att, weight, res, head_w, gate_ref, shift_ref, scale_ref, bias_ref, conv_w, bias_row, gain_row, term, landed0, landed1, final, patch, halo,
     local_sem, s1, r1, s3, r3, s5, r5, s6, r6, s7, r7,
 ):
     p = plan
     s = lax.axis_index("seq")
     h = lax.axis_index("head")
     core, across = h & 1, h >> 1
+    row_pair = (bias_row, gain_row)
 
     def slot(seq_index, head_index):
         return ((head_index & 1) * 2 + (head_index >> 1)) * p.ns + seq_index
@@ -250,14 +268,22 @@
         pltpu.make_async_copy(w_hbm, weight, local_sem.at[3]),
         pltpu.make_async_copy(res_hbm, res, local_sem.at[4]),
         pltpu.make_async_copy(hw_hbm, head_w, local_sem.at[5]),
+        pltpu.make_async_copy(gate_hbm, gate_ref, local_sem.at[9]),
+        pltpu.make_async_copy(shift_hbm, shift_ref, local_sem.at[10]),
+        pltpu.make_async_copy(scale_hbm, scale_ref, local_sem.at[11]),
+        pltpu.make_async_copy(bias_hbm, bias_ref, local_sem.at[12]),
+        pltpu.make_async_copy(cb_hbm, row_pair[0], local_sem.at[13]),
+        pltpu.make_async_copy(gain_hbm, row_pair[1], local_sem.at[14]),
     ]
+    conv_load = pltpu.make_async_copy(cw_hbm, conv_w, local_sem.at[15])
 
     def own_copies(heads):
         cols, fill = pl.ds(columns_of(s, h), heads * HEAD_DIM), pl.ds(0, heads * HEAD_DIM)
         return [
-            pltpu.make_async_copy(q_hbm.at[:, :, cols], qs.at[:, here, :, fill], local_sem.at[6]),
-            pltpu.make_async_copy(k_hbm.at[:, :, cols], kv.at[0, :, here, :, fill], local_sem.at[7]),
-            pltpu.make_async_copy(v_hbm.at[:, :, cols], kv.at[1, :, here, :, fill], local_sem.at[8]),
+            pltpu.make_async_copy(
+                ref.at[:, :, cols], got.at[i, :, here, :, fill], local_sem.at[6 + i]
+            )
+            for i, ref in enumerate((q_hbm, k_hbm, v_hbm))
         ]
 
     def by_class(end, act):
@@ -287,10 +313,14 @@
 
     def exchange(phase, index, from_slot, to_s, to_h, heads):
         cols, fill = pl.ds(columns_of(to_s, to_h), heads * HEAD_DIM), pl.ds(0, heads * HEAD_DIM)
-        if phase == 0:
-            source, target = qkv.at[pl.ds(1, 2), :, :, cols], kv.at[:, :, from_slot, :, fill]
+        if heads == p.few:
+            source, target = qkv.at[:, :, :, cols], got.at[:, :, from_slot, :, fill]
+        elif phase == 0:
+            kinds = pl.ds(1, 2)
+            source, target = qkv.at[kinds, :, :, cols], got.at[kinds, :, from_slot, :, fill]
         else:
-            source, target = qkv.at[0, phase - 1, :, cols], qs.at[phase - 1, from_slot, :, fill]
+            f = phase - 1
+            source, target = qkv.at[0, f, :, cols], got.at[0, f, from_slot, :, fill]
         return pltpu.make_async_remote_copy(
             src_ref=source,
             dst_ref=target,
@@ -300,70 +330,87 @@
             device_id_type=MESH,
         )
 
-    def for_sends(phase, act):
-        for ds in sorted(set(ds for ds, _ in offsets), key=[2, 1, 3, 0].index):
+    def for_sends(phase, heads, act):
+        for ds in range(p.ns):
             to_s = lax.rem(s + ds, p.ns)
 
-            @functools.partial(by_class, (to_s == 0) | (to_s == p.ns - 1))
-            def _(heads, ds=ds, to_s=to_s):
+            @pl.when(((to_s == 0) | (to_s == p.ns - 1)) == (heads > p.few))
+            def _():
                 for index, (ds2, dh) in enumerate(offsets):
                     if ds2 == ds:
                         act(exchange(phase, index, here, to_s, lax.rem(h + dh, p.nh), heads))
 
-    def arrivals(phase):
-        @functools.partial(by_class, at_end)
-        def _(heads):
+    def arrivals(phase, heads):
+        @pl.when(at_end == (heads > p.few))
+        def _():
             for index, (ds, dh) in enumerate(offsets):
                 from_s, from_h = lax.rem(s - ds + p.ns, p.ns), lax.rem(h - dh + p.nh, p.nh)
                 exchange(phase, index, slot(from_s, from_h), s, h, heads).wait_recv()
 
-    for phase in range(3):
-        for_sends(phase, lambda copy: copy.start())
+    stages = [(0, p.few)] + [(phase, 2 * p.few) for phase in range(1 + p.frames)]
+    for phase, heads in stages:
+        for_sends(phase, heads, lambda copy: copy.start())
+    conv_load.start()
     for copy in late:
         copy.start()
-
-    def hop(head, f, to_s, way):
+    wide_ref[...] = jnp.zeros_like(wide_ref)
+    conv_load.wait()
+    spread_weights(conv_w, wide_ref)
+
+    def hop(f, head, cut, to_s, way=0):
+        rows = p.slots * p.cells // p.cuts
+        piece = att.at[f, head, pl.ds(cut * rows, rows)]
         return pltpu.make_async_remote_copy(
-            src_ref=att.at[f, head],
-            dst_ref=att.at[f, head],
-            send_sem=s3.at[way, f, head],
-            recv_sem=r3.at[f, head],
+            src_ref=piece,
+            dst_ref=piece,
+            send_sem=s3.at[way, f, head, cut],
+            recv_sem=r3.at[f, head, cut],
             device_id={"seq": to_s},
             device_id_type=MESH,
         )
 
     def attend(f, j):
         lanes = slice(j * HEAD_DIM, (j + 1) * HEAD_DIM)
-        q = qs[f, :, :, lanes].reshape(-1, HEAD_DIM)
-        k = kv[0, :, :, :, lanes].reshape(-1, HEAD_DIM)
-        v = kv[1, :, :, :, lanes].reshape(-1, HEAD_DIM)
+        q = got[0, f, :, :, lanes].reshape(-1, HEAD_DIM)
+        k = got[1, :, :, :, lanes].reshape(-1, HEAD_DIM)
+        v = got[2, :, :, :, lanes].reshape(-1, HEAD_DIM)
         scores = lax.dot_general(
             q, k, (((1,), (1,)), ((), ())), preferred_element_type=jnp.float32
         )
-        scores = scores * HEAD_DIM ** (-0.5)
-        weights = jnp.exp(scores - jnp.max(scores, -1, keepdims=True))
+        scale = HEAD_DIM ** (-0.5) * math.log2(math.e)
+        weights = jnp.exp2((scores - jnp.max(scores, -1, keepdims=True)) * scale)
         denominator = jnp.sum(weights, -1, keepdims=True)
         product = jnp.dot(weights.astype(jnp.bfloat16), v, preferred_element_type=jnp.float32)
         att[f, p.few * (s + jnp.minimum(s, 1)) + j] = (product / denominator).astype(jnp.bfloat16)
 
+    def targets(head, row):
+        o = p.owner[head]
+        rows = [r for r in range(p.ns) if r != o and source_row(o, head - p.owner.index(o), r) == row]
+        return sorted(rows, key=lambda r: -abs(r - row))
+
+    def hand_on(f, head, row, way):
+        rows = targets(head, row)
+        if way < len(rows):
+            for cut in range(p.cuts):
+                hop(f, head, cut, rows[way], way).start()
+
     def send_own(f, j, way):
-        for o in range(p.ns):
-            if j < p.counts[o]:
-                head = p.owner.index(o) + j
-
-                @pl.when(s == o)
+        for row in range(p.ns):
+            if j < p.counts[row]:
+
+                @pl.when(s == row)
                 def _():
-                    hop(head, f, SENDS[o][way], way).start()
-
+                    hand_on(f, p.owner.index(row) + j, row, way)
+
+    @functools.partial(by_class, at_end)
+    def _(heads):
+        for copy in own_copies(heads):
+            copy.wait()
+
+    arrivals(0, p.few)
+    arrivals(0, 2 * p.few)
     for f in range(p.frames):
-        if f == 0:
-            @functools.partial(by_class, at_end)
-            def _(heads):
-                for copy in own_copies(heads):
-                    copy.wait()
-
-            arrivals(0)
-        arrivals(1 + f)
+        arrivals(1 + f, 2 * p.few)
         for j in range(p.few):
             attend(f, j)
             send_own(f, j, 0)
@@ -373,43 +420,38 @@
                 attend(f, j)
 
             send_own(f, j, 0)
+        for j in range(p.few):
+            pl.when(jnp.logical_not(at_end))(functools.partial(send_own, f, j, 1))
+    for f in range(p.frames):
         for j in range(2 * p.few):
-            send_own(f, j, 1)
+            pl.when(at_end)(functools.partial(send_own, f, j, 1))
 
     def order(row):
-        others = [head for head in range(p.group) if p.owner[head] != row]
-        relayed = {head: row == RELAY[p.owner[head]][0] for head in others}
-        return sorted(
-            others,
-            key=lambda head: (
-                abs(p.owner[head] - row) if relayed[head] or row in (0, p.ns - 1) else 9, head,
-            ),
-        )
-
-    def take(f, head, row):
-        hop(head, f, row, 0).wait_recv()
-        relay, last = RELAY[p.owner[head]]
-        if row == relay:
-            hop(head, f, last, 0).start()
+        def when(item):
+            f, head = item
+            o = p.owner[head]
+            return (due(o, head - p.owner.index(o), f, row), f, head)
+
+        every = [(f, head) for f in range(p.frames) for head in range(p.group)]
+        return sorted((item for item in every if p.owner[item[1]] != row), key=when)
+
+    def first_part(row):
+        items = order(row)
+        last = max(i for i, (f, _) in enumerate(items) if f == 0)
+        return items[: last + 1]
+
+    def second_part(row):
+        return order(row)[len(first_part(row)) :]
 
     def gather(todo):
         for row in range(p.ns):
             @pl.when(s == row)
             def _():
                 for f, head in todo(row):
-                    take(f, head, row)
-
-    def first_part(row):
-        heads = order(row)
-        near = [head for head in heads if abs(p.owner[head] - row) == 1 and p.owner[head] in (1, 2)]
-        early = near if row in (1, 2) else []
-        return [(0, head) for head in early] + [(1, head) for head in early] + [
-            (0, head) for head in heads if head not in early
-        ]
-
-    def second_part(row):
-        done = first_part(row)
-        return [(1, head) for head in order(row) if (1, head) not in done]
+                    for cut in range(p.cuts):
+                        hop(f, head, cut, row).wait_recv()
+                        for way, to_s in enumerate(targets(head, row)):
+                            hop(f, head, cut, to_s, way).start()
 
     def halving(f, c, b):
         bit = core if b == 0 else across
@@ -424,12 +466,17 @@
             device_id_type=MESH,
         )
 
-    def project(f, c):
-        cols = pl.ds(c * p.chunk, p.chunk)
+    groups = [range(2), range(2, p.chunks)] if p.chunks > 3 else [range(p.chunks)]
+
+    def project(f):
         rows = jnp.concatenate([att[f, head] for head in range(p.group)], axis=1)
-        product = jnp.dot(rows, weight[:, cols], preferred_element_type=jnp.float32)
-        term[f, c] = product.astype(jnp.bfloat16).reshape(term.shape[2:])
-        halving(f, c, 0).start()
+        for group in groups:
+            for c in group:
+                cols = pl.ds(c * p.chunk, p.chunk)
+                product = jnp.dot(rows, weight[:, cols], preferred_element_type=jnp.float32)
+                term[f, c] = product.astype(jnp.bfloat16).reshape(term.shape[2:])
+            for c in group:
+                halving(f, c, 0).start()
 
     def pair_sum(f, c):
         halving(f, c, 0).wait_recv()
@@ -458,18 +505,22 @@
 
     gather(first_part)
     late[0].wait()
-    for c in range(p.chunks):
-        project(0, c)
-    for c in range(p.chunks):
-        pair_sum(0, c)
+    project(0)
+    def pair_sums():
+        for c in range(p.chunks):
+            pair_sum(0, c)
+
+    pl.when(at_end)(pair_sums)
     gather(second_part)
-    for c in range(p.chunks):
-        project(1, c)
+    pl.when(jnp.logical_not(at_end))(pair_sums)
+    project(1)
     for c in range(p.chunks):
         pair_sum(1, c)
         full_sum(0, c)
     for copy in late[1:]:
         copy.wait()
+    for i, row in enumerate(row_pair):
+        rows_ref[i] = row[...]
 
     def finish(f, c, sums):
         for ds in range(1, p.ns):
@@ -503,6 +554,7 @@
     features = values.shape[-1]
     patch[...] = jnp.zeros_like(patch)
     patch[:, :features] = values
+    blank = jnp.zeros(patch.shape, patch.dtype)
 
     moves = [(0, 1), (0, -1), (1, 0), (1, 1), (1, -1)]
 
@@ -530,17 +582,17 @@
         def _():
             reach(index).start()
 
-    near_ref[1, 1] = values
+    near_ref[1, 1] = patch[...]
     for index, (dh, ds) in enumerate(moves):
 
         @pl.when(edge(index, -1))
         def _():
             reach(index).wait_recv()
-            near_ref[1 - dh, 1 - ds] = halo[index][:, :features]
+            near_ref[1 - dh, 1 - ds] = halo[index]
 
         @pl.when(jnp.logical_not(edge(index, -1)))
         def _():
-            near_ref[1 - dh, 1 - ds] = jnp.zeros_like(values)
+            near_ref[1 - dh, 1 - ds] = blank
 
     for index in range(len(moves)):
 
@@ -548,20 +600,17 @@
         def _():
             reach(index).wait_send()
 
-    for phase in range(3):
-        for_sends(phase, lambda copy: copy.wait_send())
+    for phase, heads in stages:
+        for_sends(phase, heads, lambda copy: copy.wait_send())
 
     for row in range(p.ns):
         @pl.when(s == row)
         def _():
             for f in range(p.frames):
                 for head in range(p.group):
-                    o = p.owner[head]
-                    if o == row:
-                        for way in range(2):
-                            hop(head, f, SENDS[o][way], way).wait_send()
-                    elif RELAY[o][0] == row:
-                        hop(head, f, RELAY[o][1], 0).wait_send()
+                    for way, to_s in enumerate(targets(head, row)):
+                        for cut in range(p.cuts):
+                            hop(f, head, cut, to_s, way).wait_send()
 
     for f in range(p.frames):
         for c in range(p.chunks):
@@ -569,6 +618,77 @@
                 halving(f, c, b).wait_send()
             for ds in range(1, p.ns):
                 to_owner(f, c, ds, s).wait_send()
+
+
+def spread_weights(conv_w, wide_ref):
+    taps, depth, channels = conv_w.shape
+    part = depth // 3
+    for a in range(2):
+        for dt in range(3):
+            for dy in range(3):
+                base = (1 - a + dy) * 4 * part
+                tap = conv_w[dt * 3 + dy]
+                wide_ref[a, dt, base : base + depth, :channels] = tap
+                wide_ref[a, dt, base + part : base + part + depth, channels:] = tap
+
+
+def conv_kernel(
+    cells, hidden_ref, near_ref, wide_ref, rows_ref, hidden_out, features_out, mixed, features, sems
+):
+    tokens = near_ref.shape[2]
+    lanes = near_ref.shape[3]
+    part = lanes // 8
+    channels = features.shape[-1]
+    hidden_copy = pltpu.make_async_copy(hidden_ref, hidden_out, sems.at[0])
+    hidden_copy.start()
+
+    values = near_ref[...].reshape(-1, lanes).astype(jnp.float32)
+    total = values.shape[0]
+    column = lax.broadcasted_iota(jnp.int32, values.shape, 0) % cells
+    left = jnp.where(column == 0, 0.0, pltpu.roll(values, 1, 0))
+    right = jnp.where(column == cells - 1, 0.0, pltpu.roll(values, total - 1, 0))
+
+    source = lax.broadcasted_iota(jnp.int32, (lanes, lanes), 0)
+    target = lax.broadcasted_iota(jnp.int32, (lanes, lanes), 1)
+    upper, place = target // (4 * part), target % (4 * part)
+    start = upper * 2 * part
+
+    def moved(x, low, high, first):
+        pick = (place >= low * part) & (place < high * part)
+        pick = pick & (source == start + place + (first - low) * part)
+        matrix = jnp.where(pick, 1.0, 0.0).astype(jnp.bfloat16)
+        return jnp.dot(x.astype(jnp.bfloat16), matrix, preferred_element_type=jnp.float32)
+
+    strip = moved(left, 0, 1, 1) + moved(values, 1, 3, 0) + moved(right, 3, 4, 0)
+    strip = strip.reshape(2, 3, tokens, lanes).astype(jnp.bfloat16)
+
+    def at_time(dt, row):
+        if dt == 1:
+            return jnp.concatenate([strip[0, row, cells:], strip[1, row, :cells]], axis=0)
+        return strip[dt // 2, row]
+
+    for a in range(2):
+        taken = [at_time(dt, row) for dt in range(3) for row in (a, a + 1)]
+        linear = jnp.dot(
+            jnp.concatenate(taken, axis=1),
+            wide_ref[a].reshape(-1, 2 * channels),
+            preferred_element_type=jnp.float32,
+        )
+        for b in range(2):
+            value = linear[:, b * channels : (b + 1) * channels] + rows_ref[0:1]
+            square = jnp.mean(value * value, -1, keepdims=True)
+            value = value * lax.rsqrt(square + 1e-06) * rows_ref[1:2]
+            value = value / (1.0 + jnp.exp(-value))
+            for k in range(channels // 128):
+                for f in range(2):
+                    piece = value[f * cells : (f + 1) * cells, k * 128 : (k + 1) * 128]
+                    mixed[k, f, a, pl.ds(b, cells, 2)] = piece
+    for k in range(channels // 128):
+        features[:, :, :, k * 128 : (k + 1) * 128] = mixed[k].astype(jnp.bfloat16)
+    features_copy = pltpu.make_async_copy(features, features_out, sems.at[1])
+    features_copy.start()
+    hidden_copy.wait()
+    features_copy.wait()
 
 
 def on_device(
@@ -588,7 +708,7 @@
 ):
     ns, nh = lax.axis_size("seq"), lax.axis_size("head")
     p = Plan(ns, nh, queries, residual, out_weight)
-    if not p.fits(queries):
+    if not p.fits(queries, head_weight, conv_weight):
         return on_device_gathered(
             queries, attn_keys, attn_values, residual, out_weight, out_gate, head_shift,
             head_scale, head_weight, head_bias, conv_weight, conv_bias, norm_gain,
@@ -598,35 +718,44 @@
     dma, bf16 = pltpu.SemaphoreType.DMA, jnp.bfloat16
     lanes = -(-patch_size // 128) * 128
     most = 2 * p.few * HEAD_DIM
-    any_spec = pl.BlockSpec(memory_space=pl.ANY)
+    channels = conv_weight.shape[-1]
+    hbm = pl.BlockSpec(memory_space=pltpu.HBM)
     vmem = pl.BlockSpec(memory_space=pltpu.VMEM)
-    hidden, near = pl.pallas_call(
+    hidden, near, wide, conv_rows = pl.pallas_call(
         functools.partial(block_kernel, p),
         out_shape=(
             jax.ShapeDtypeStruct((t, width), bf16),
-            jax.ShapeDtypeStruct((2, 3, t, patch_size), bf16),
+            jax.ShapeDtypeStruct((2, 3, t, lanes), bf16),
+            jax.ShapeDtypeStruct((2, 3, 2 * lanes, 2 * channels), bf16),
+            jax.ShapeDtypeStruct((2, channels), jnp.float32),
         ),
-        in_specs=[any_spec] * 6 + [vmem] * 4,
-        out_specs=(vmem, vmem),
+        in_specs=[hbm] * 13,
+        out_specs=(vmem,) * 4,
         scratch_shapes=[
             pltpu.VMEM((3, frames, cells, inner), bf16),
-            pltpu.VMEM((frames, p.slots, cells, most), bf16),
-            pltpu.VMEM((2, frames, p.slots, cells, most), bf16),
+            pltpu.VMEM((3, frames, p.slots, cells, most), bf16),
             pltpu.VMEM((frames, p.group, p.slots * cells, HEAD_DIM), bf16),
             pltpu.VMEM(out_weight.shape, bf16),
             pltpu.VMEM((t, width), bf16),
             pltpu.VMEM(head_weight.shape[::-1], bf16),
+            pltpu.VMEM((1, width), jnp.float32),
+            pltpu.VMEM((1, width), jnp.float32),
+            pltpu.VMEM((1, width), jnp.float32),
+            pltpu.VMEM((1, patch_size), jnp.float32),
+            pltpu.VMEM((9, 3 * conv_weight.shape[3], channels), bf16),
+            pltpu.VMEM((channels,), jnp.float32),
+            pltpu.VMEM((channels,), jnp.float32),
             pltpu.VMEM((frames, p.chunks, 2, 2, ns, cells, p.chunk), bf16),
             pltpu.VMEM((frames, p.chunks, 2, ns, cells, p.chunk), bf16),
             pltpu.VMEM((frames, p.chunks, ns, cells, p.chunk), bf16),
             pltpu.VMEM((frames, p.chunks, ns, cells, p.chunk), bf16),
             pltpu.VMEM((t, lanes), bf16),
             pltpu.VMEM((5, t, lanes), bf16),
-            dma((9,)),
+            dma((16,)),
             dma((3, p.slots - 1)),
             dma((3, p.slots - 1)),
-            dma((2, frames, p.group)),
-            dma((frames, p.group)),
+            dma((2, frames, p.group, p.cuts)),
+            dma((frames, p.group, p.cuts)),
             dma((2, frames, p.chunks)),
             dma((2, frames, p.chunks)),
             dma((ns - 1, frames, p.chunks)),
@@ -635,9 +764,9 @@
             dma((5,)),
         ],
         compiler_params=pltpu.CompilerParams(
-            collective_id=0, has_side_effects=True, vmem_limit_bytes=60 * 1024 * 1024
+            collective_id=0, has_side_effects=True, vmem_limit_bytes=16 * 1024 * 1024
         ),
-    )(
+    )(*(pltpu.with_memory_space_constraint(x, pltpu.HBM) for x in (
         queries.reshape(frames, cells, inner),
         attn_keys.reshape(frames, cells, inner),
         attn_values.reshape(frames, cells, inner),
@@ -648,16 +777,25 @@
         head_shift.reshape(1, -1),
         head_scale.reshape(1, -1),
         head_bias.reshape(1, -1),
-    )
-    channels = patch_size // 4
-    video = near.reshape(2, 3, frames, height, breadth, 2, 2, channels)
-    video = video.transpose(0, 2, 1, 3, 5, 4, 6, 7)
-    video = video.reshape(2, frames, 3 * height * 2, breadth * 2, channels)
-    video = jnp.concatenate([video[0, -2:], video[1]], 0)
-    rows = height * 2
-    video = video[:, rows - 1 : 2 * rows + 1]
-    padded = jnp.pad(video, ((0, 0), (0, 0), (1, 1), (0, 0)))
-    features = convolve(padded, frames, conv_weight, conv_bias, norm_gain)
+        conv_weight.reshape(9, -1, channels),
+        conv_bias,
+        norm_gain,
+    )))
+    hidden, features = pl.pallas_call(
+        functools.partial(conv_kernel, cells),
+        out_shape=(
+            jax.ShapeDtypeStruct((t, width), bf16),
+            jax.ShapeDtypeStruct((frames, 2, 2 * cells, channels), bf16),
+        ),
+        in_specs=[vmem] * 4,
+        out_specs=(hbm, hbm),
+        scratch_shapes=[
+            pltpu.VMEM((channels // 128, frames, 2, 2 * cells, 128), jnp.float32),
+            pltpu.VMEM((frames, 2, 2 * cells, channels), bf16),
+            dma((2,)),
+        ],
+        compiler_params=pltpu.CompilerParams(vmem_limit_bytes=8 * 1024 * 1024),
+    )(hidden, near, wide, conv_rows)
     return (hidden.reshape(residual.shape), features)
 
 

time: 62.1 us -> 54 us (0.87)
  local copies, waits for them, and re-layouts: 3.45 us -> 0 us
  Pallas kernels: 56.4 us -> 53.2 us
  other arithmetic: 0.84 us -> 0 us
    pallas_call x1, Pallas kernels: 56.4 us -> 51.7 us  [on_device(): pl.pallas_call(functools.partial(block_kernel, p), out_shape=(jax.ShapeDt...]
    unnamed x9 -> x0, local copies, waits for them, and re-layouts: 1.71 us -> none
    pallas_call x0 -> x1, Pallas kernels: none -> 1.49 us  [on_device(): pl.pallas_call(functools.partial(conv_kernel, cells), out_shape=(jax.Shap...]
    reshape x2 -> x0, local copies, waits for them, and re-layouts: 1.1 us -> none  [on_device(): video = near.reshape(2, 3, frames, height, breadth, 2, 2, channels)]
    convert_element_type x1 -> x0, other arithmetic: 0.78 us -> none  [convolve(): jax.nn.silu(normed).astype(jnp.bfloat16)]
where the time goes in v2:
time: 54 us; the launch traced here: 53.8 us
  Pallas kernels  53.2 us (99%)
  between operations  0.64 us (1%)
    pallas_call x1, Pallas kernels, on_device(): pl.pallas_call(functools.partial(block_kernel, p), out_shape=(jax.ShapeDt...  51.7 us
    pallas_call x1, Pallas kernels, on_device(): pl.pallas_call(functools.partial(conv_kernel, cells), out_shape=(jax.Shap...  1.49 us

profile of v2, /device:TPU:0, one launch (start us, length us, event | category | flops | bytes accessed | tf_op | source)
XLA Modules:
  0.0 53.8 jit_solution(9855066477223275160)
XLA Ops:
  0.6 51.7 %shard_map.140 = (bf16[32,5120]{1,0:T(8,128)(2,1)S(1)}, bf16[2,3,32,128]{3,2,1,0:T(8,128)(2,1)S(1)}, bf16[2,3,256,768]{3,2,1,0:T(8,128)(2,1)S(1)}, f32[2,384]{1,0:T(2,128)S(1)}) custom-call(bf16[2,16,3072]{2,1,0:T(8,128)(2,1)} %bitcast.16, bf16[2,16,3072]{2,1,0:T(8,128)(2,1)} %bitcast.17, bf16[2,16,3072]{2,1,0:T(8,128)(2,1)} %bitcast.18, ...), custom_call_target="tpu_custom_call" | custom-call | tf_op jit(solution)/shard_map/pallas_call | solution.py:724
  52.3 1.5 %shard_map.141 = (bf16[32,5120]{1,0:T(8,128)(2,1)}, bf16[2,2,32,384]{3,2,1,0:T(8,128)(2,1)}) custom-call(bf16[32,5120]{1,0:T(8,128)(2,1)S(1)} %get-tuple-element.8.hidden_ref, bf16[2,3,32,128]{3,2,1,0:T(8,128)(2,1)S(1)} %get-tuple-element.9.near_ref, bf16[2,3,256,768]{3,2,1,0:T(8,128)(2,1)S(1)} %get-tuple-element.10.wide_ref, ...), custom_call_target="tpu_custom_call" | custom-call | tf_op jit(solution)/shard_map/pallas_call | solution.py:784

commit v3 on v2

--- a/solution.py
+++ b/solution.py
@@ -197,7 +197,7 @@
         self.chunk = 256 if self.columns % 256 == 0 else 128
         self.chunks = self.columns // self.chunk
         self.cuts = 2
-        self.counts = (2 * self.few, self.few, self.few, 2 * self.few)
+        self.counts = (self.few, 2 * self.few, 2 * self.few, self.few)
         self.owner = [o for o, count in enumerate(self.counts) for _ in range(count)]
 
     def fits(self, queries, head_weight, conv_weight):
@@ -217,20 +217,18 @@
         )
 
 
-def source_row(o, j, row):
+def source_row(o, row):
     step = 1 if row > o else -1
-    if o in (1, 2) or j % 2 == 0:
-        return row - step
-    return o if abs(row - o) < 3 else row - step
-
-
-def due(o, j, f, row):
+    return o if o in (0, 3) and abs(row - o) < 3 else row - step
+
+
+def due(o, unit, f, row):
     away = abs(row - o)
-    if o in (1, 2):
-        return 3.0 * away
-    if j % 2 == 0:
-        return 14.4 + 2.8 * f + 2.8 * away
-    return 20.4 + 1.4 * f + 2.4 if away == 1 else 16.7 + 2.8 * f + 2.8 * (away - 1)
+    if o in (0, 3):
+        return (0, 15.0, 15.5, 18.5)[away] + 1.5 * f
+    if row == 3 * (o // 2):
+        return (10.0, 18.0)[unit] + 1.4 * f
+    return (15.7, 19.4)[unit] + 3.0 * (away - 1) + 1.4 * f
 
 
 def block_kernel(
@@ -239,7 +237,7 @@
     gate_hbm, shift_hbm, scale_hbm, bias_hbm, cw_hbm, cb_hbm, gain_hbm,
     hidden_ref, near_ref, wide_ref, rows_ref,
     qkv, got, att, weight, res, head_w, gate_ref, shift_ref, scale_ref, bias_ref, conv_w, bias_row, gain_row, term, landed0, landed1, final, patch, halo,
-    local_sem, s1, r1, s3, r3, s5, r5, s6, r6, s7, r7,
+    load_sem, local_sem, own_sem, s1, r1, s3, r3, s4, r4, s5, r5, s6, r6, s7, r7,
 ):
     p = plan
     s = lax.axis_index("seq")
@@ -252,43 +250,39 @@
 
     here = slot(s, h)
     at_end = (s == 0) | (s == p.ns - 1)
-    offsets = [(ds, dh) for ds in (2, 1, 3, 0) for dh in range(p.nh) if ds or dh]
-    widths = ((2 * p.few, True), (p.few, False))
-
-    def columns_of(seq_index, head_index):
-        before = p.few * (seq_index + jnp.minimum(seq_index, 1))
-        return pl.multiple_of((head_index * p.group + before) * HEAD_DIM, HEAD_DIM)
-
-    loads = [
-        pltpu.make_async_copy(q_hbm, qkv.at[0], local_sem.at[0]),
-        pltpu.make_async_copy(k_hbm, qkv.at[1], local_sem.at[1]),
-        pltpu.make_async_copy(v_hbm, qkv.at[2], local_sem.at[2]),
+    offsets = [(ds, dh) for ds in range(p.ns) for dh in range(p.nh) if ds or dh]
+    wide = p.few * HEAD_DIM
+
+    def columns_of(seq_index, head_index, unit):
+        before = p.few * (jnp.maximum(2 * seq_index - 1, 0) + unit)
+        return pl.ds(pl.multiple_of((head_index * p.group + before) * HEAD_DIM, HEAD_DIM), wide)
+
+    sources = (q_hbm, k_hbm, v_hbm)
+    loads = [pltpu.make_async_copy(ref, qkv.at[i], load_sem) for i, ref in enumerate(sources)]
+    loaded = pltpu.make_async_copy(qkv, qkv, load_sem)
+    late = [
+        pltpu.make_async_copy(w_hbm, weight, local_sem.at[0]),
+        pltpu.make_async_copy(res_hbm, res, local_sem.at[1]),
+        pltpu.make_async_copy(hw_hbm, head_w, local_sem.at[2]),
+        pltpu.make_async_copy(gate_hbm, gate_ref, local_sem.at[3]),
+        pltpu.make_async_copy(shift_hbm, shift_ref, local_sem.at[4]),
+        pltpu.make_async_copy(scale_hbm, scale_ref, local_sem.at[5]),
+        pltpu.make_async_copy(bias_hbm, bias_ref, local_sem.at[6]),
+        pltpu.make_async_copy(cb_hbm, row_pair[0], local_sem.at[7]),
+        pltpu.make_async_copy(gain_hbm, row_pair[1], local_sem.at[8]),
     ]
-    late = [
-        pltpu.make_async_copy(w_hbm, weight, local_sem.at[3]),
-        pltpu.make_async_copy(res_hbm, res, local_sem.at[4]),
-        pltpu.make_async_copy(hw_hbm, head_w, local_sem.at[5]),
-        pltpu.make_async_copy(gate_hbm, gate_ref, local_sem.at[9]),
-        pltpu.make_async_copy(shift_hbm, shift_ref, local_sem.at[10]),
-        pltpu.make_async_copy(scale_hbm, scale_ref, local_sem.at[11]),
-        pltpu.make_async_copy(bias_hbm, bias_ref, local_sem.at[12]),
-        pltpu.make_async_copy(cb_hbm, row_pair[0], local_sem.at[13]),
-        pltpu.make_async_copy(gain_hbm, row_pair[1], local_sem.at[14]),
-    ]
-    conv_load = pltpu.make_async_copy(cw_hbm, conv_w, local_sem.at[15])
-
-    def own_copies(heads):
-        cols, fill = pl.ds(columns_of(s, h), heads * HEAD_DIM), pl.ds(0, heads * HEAD_DIM)
+    conv_load = pltpu.make_async_copy(cw_hbm, conv_w, local_sem.at[9])
+
+    def own_copies(unit):
+        cols = columns_of(s, h, unit)
         return [
-            pltpu.make_async_copy(
-                ref.at[:, :, cols], got.at[i, :, here, :, fill], local_sem.at[6 + i]
-            )
-            for i, ref in enumerate((q_hbm, k_hbm, v_hbm))
+            pltpu.make_async_copy(ref.at[:, :, cols], got.at[unit, i, :, here], own_sem.at[unit])
+            for i, ref in enumerate(sources)
         ]
 
-    def by_class(end, act):
-        for heads, wanted in widths:
-            pl.when(end == wanted)(functools.partial(act, heads))
+    def own_copied(unit):
+        part = got.at[unit, :, :, here]
+        return pltpu.make_async_copy(part, part, own_sem.at[unit])
 
     for copy in loads:
         copy.start()
@@ -301,55 +295,42 @@
             device_id={"seq": lax.rem(s + ds, p.ns), "head": lax.rem(h + dh, p.nh)},
             device_id_type=MESH,
         )
-
-    @functools.partial(by_class, at_end)
-    def _(heads):
-        for copy in own_copies(heads):
+    for copy in own_copies(0):
+        copy.start()
+
+    @pl.when(jnp.logical_not(at_end))
+    def _():
+        for copy in own_copies(1):
             copy.start()
 
-    for copy in loads:
-        copy.wait()
+    loaded.wait()
     pl.semaphore_wait(barrier, len(offsets))
 
-    def exchange(phase, index, from_slot, to_s, to_h, heads):
-        cols, fill = pl.ds(columns_of(to_s, to_h), heads * HEAD_DIM), pl.ds(0, heads * HEAD_DIM)
-        if heads == p.few:
-            source, target = qkv.at[:, :, :, cols], got.at[:, :, from_slot, :, fill]
-        elif phase == 0:
-            kinds = pl.ds(1, 2)
-            source, target = qkv.at[kinds, :, :, cols], got.at[kinds, :, from_slot, :, fill]
-        else:
-            f = phase - 1
-            source, target = qkv.at[0, f, :, cols], got.at[0, f, from_slot, :, fill]
+    def exchange(stage, to_s, to_h):
+        unit = stage // 2
         return pltpu.make_async_remote_copy(
-            src_ref=source,
-            dst_ref=target,
-            send_sem=s1.at[phase, index],
-            recv_sem=r1.at[phase, index],
+            src_ref=qkv.at[:, :, :, columns_of(to_s, to_h, unit)],
+            dst_ref=got.at[unit, :, :, here],
+            send_sem=s1,
+            recv_sem=r1.at[stage],
             device_id={"seq": to_s, "head": to_h},
             device_id_type=MESH,
         )
 
-    def for_sends(phase, heads, act):
+    for stage in (1, 0, 2):
         for ds in range(p.ns):
             to_s = lax.rem(s + ds, p.ns)
 
-            @pl.when(((to_s == 0) | (to_s == p.ns - 1)) == (heads > p.few))
+            @pl.when(((to_s == 0) | (to_s == p.ns - 1)) == (stage == 0))
             def _():
-                for index, (ds2, dh) in enumerate(offsets):
+                for ds2, dh in offsets:
                     if ds2 == ds:
-                        act(exchange(phase, index, here, to_s, lax.rem(h + dh, p.nh), heads))
-
-    def arrivals(phase, heads):
-        @pl.when(at_end == (heads > p.few))
-        def _():
-            for index, (ds, dh) in enumerate(offsets):
-                from_s, from_h = lax.rem(s - ds + p.ns, p.ns), lax.rem(h - dh + p.nh, p.nh)
-                exchange(phase, index, slot(from_s, from_h), s, h, heads).wait_recv()
-
-    stages = [(0, p.few)] + [(phase, 2 * p.few) for phase in range(1 + p.frames)]
-    for phase, heads in stages:
-        for_sends(phase, heads, lambda copy: copy.start())
+                        exchange(stage, to_s, lax.rem(h + dh, p.nh)).start()
+
+    def arrived(stage):
+        parts = got.at[stage // 2, :, :, pl.ds(0, p.slots - 1)]
+        pltpu.make_async_copy(parts, parts, r1.at[stage]).wait()
+
     conv_load.start()
     for copy in late:
         copy.start()
@@ -357,23 +338,23 @@
     conv_load.wait()
     spread_weights(conv_w, wide_ref)
 
-    def hop(f, head, cut, to_s, way=0):
+    def hop(f, head, cut, to_s, relayed):
         rows = p.slots * p.cells // p.cuts
         piece = att.at[f, head, pl.ds(cut * rows, rows)]
         return pltpu.make_async_remote_copy(
             src_ref=piece,
             dst_ref=piece,
-            send_sem=s3.at[way, f, head, cut],
+            send_sem=s3.at[relayed],
             recv_sem=r3.at[f, head, cut],
             device_id={"seq": to_s},
             device_id_type=MESH,
         )
 
     def attend(f, j):
-        lanes = slice(j * HEAD_DIM, (j + 1) * HEAD_DIM)
-        q = got[0, f, :, :, lanes].reshape(-1, HEAD_DIM)
-        k = got[1, :, :, :, lanes].reshape(-1, HEAD_DIM)
-        v = got[2, :, :, :, lanes].reshape(-1, HEAD_DIM)
+        unit, lanes = j // p.few, pl.ds(j % p.few * HEAD_DIM, HEAD_DIM)
+        q = got[unit, 0, f, :, :, lanes].reshape(-1, HEAD_DIM)
+        k = got[unit, 1, :, :, :, lanes].reshape(-1, HEAD_DIM)
+        v = got[unit, 2, :, :, :, lanes].reshape(-1, HEAD_DIM)
         scores = lax.dot_general(
             q, k, (((1,), (1,)), ((), ())), preferred_element_type=jnp.float32
         )
@@ -381,129 +362,131 @@
         weights = jnp.exp2((scores - jnp.max(scores, -1, keepdims=True)) * scale)
         denominator = jnp.sum(weights, -1, keepdims=True)
         product = jnp.dot(weights.astype(jnp.bfloat16), v, preferred_element_type=jnp.float32)
-        att[f, p.few * (s + jnp.minimum(s, 1)) + j] = (product / denominator).astype(jnp.bfloat16)
+        att[f, p.few * jnp.maximum(2 * s - 1, 0) + j] = (product / denominator).astype(jnp.bfloat16)
 
     def targets(head, row):
         o = p.owner[head]
-        rows = [r for r in range(p.ns) if r != o and source_row(o, head - p.owner.index(o), r) == row]
+        rows = [r for r in range(p.ns) if r != o and source_row(o, r) == row]
         return sorted(rows, key=lambda r: -abs(r - row))
 
-    def hand_on(f, head, row, way):
-        rows = targets(head, row)
-        if way < len(rows):
-            for cut in range(p.cuts):
-                hop(f, head, cut, rows[way], way).start()
-
-    def send_own(f, j, way):
+    def send_own(f, j):
         for row in range(p.ns):
             if j < p.counts[row]:
+                head = p.owner.index(row) + j
 
                 @pl.when(s == row)
                 def _():
-                    hand_on(f, p.owner.index(row) + j, row, way)
-
-    @functools.partial(by_class, at_end)
-    def _(heads):
-        for copy in own_copies(heads):
-            copy.wait()
-
-    arrivals(0, p.few)
-    arrivals(0, 2 * p.few)
-    for f in range(p.frames):
-        arrivals(1 + f, 2 * p.few)
-        for j in range(p.few):
-            attend(f, j)
-            send_own(f, j, 0)
-        for j in range(p.few, 2 * p.few):
-            @pl.when(at_end)
-            def _():
-                attend(f, j)
-
-            send_own(f, j, 0)
-        for j in range(p.few):
-            pl.when(jnp.logical_not(at_end))(functools.partial(send_own, f, j, 1))
-    for f in range(p.frames):
-        for j in range(2 * p.few):
-            pl.when(at_end)(functools.partial(send_own, f, j, 1))
+                    for to_s in targets(head, row):
+                        for cut in range(p.cuts):
+                            hop(f, head, cut, to_s, 0).start()
 
     def order(row):
         def when(item):
             f, head = item
             o = p.owner[head]
-            return (due(o, head - p.owner.index(o), f, row), f, head)
+            return (f, due(o, (head - p.owner.index(o)) // p.few, f, row), head)
 
         every = [(f, head) for f in range(p.frames) for head in range(p.group)]
         return sorted((item for item in every if p.owner[item[1]] != row), key=when)
 
-    def first_part(row):
-        items = order(row)
-        last = max(i for i, (f, _) in enumerate(items) if f == 0)
-        return items[: last + 1]
-
-    def second_part(row):
-        return order(row)[len(first_part(row)) :]
+    def take(f, head, row):
+        for cut in range(p.cuts):
+            hop(f, head, cut, row, 1).wait_recv()
+            for to_s in targets(head, row):
+                hop(f, head, cut, to_s, 1).start()
 
     def gather(todo):
         for row in range(p.ns):
             @pl.when(s == row)
             def _():
                 for f, head in todo(row):
-                    for cut in range(p.cuts):
-                        hop(f, head, cut, row).wait_recv()
-                        for way, to_s in enumerate(targets(head, row)):
-                            hop(f, head, cut, to_s, way).start()
-
-    def halving(f, c, b):
-        bit = core if b == 0 else across
-        source = term.at[f, c, 1 - bit] if b == 0 else landed0.at[f, c, 1 - bit]
-        target = landed0.at[f, c] if b == 0 else landed1.at[f, c]
+                    take(f, head, row)
+
+    def early_part(row):
+        def early(f, head):
+            unit = (head - p.owner.index(p.owner[head])) // p.few
+            return f == 0 and unit == 0 and row in (1, 2) and targets(head, row)
+
+        return [item for item in order(row) if early(*item)]
+
+    def part(f, row):
+        return [item for item in order(row) if item[0] == f and item not in early_part(row)]
+
+    own_copied(0).wait()
+    pl.when(at_end)(functools.partial(arrived, 0))
+    pl.when(jnp.logical_not(at_end))(functools.partial(arrived, 1))
+    for f in range(p.frames):
+        for j in range(p.few):
+            attend(f, j)
+            send_own(f, j)
+
+    @pl.when(jnp.logical_not(at_end))
+    def _():
+        own_copied(1).wait()
+        arrived(2)
+        for f in range(p.frames):
+            for j in range(p.few, 2 * p.few):
+                attend(f, j)
+                send_own(f, j)
+            if f == 0:
+                gather(early_part)
+
+    groups = [(0, 2), (2, p.chunks - 2)] if p.chunks > 3 else [(0, p.chunks)]
+
+    def to_partner(f, g):
+        part = pl.ds(*groups[g])
         return pltpu.make_async_remote_copy(
-            src_ref=source,
-            dst_ref=target,
-            send_sem=s5.at[b, f, c],
-            recv_sem=r5.at[b, f, c],
-            device_id={"head": h + (1 - 2 * bit) * (1 << b)},
+            src_ref=term.at[f, part, 1 - core],
+            dst_ref=landed0.at[f, part],
+            send_sem=s4,
+            recv_sem=r4.at[f, g],
+            device_id={"head": h + 1 - 2 * core},
             device_id_type=MESH,
         )
-
-    groups = [range(2), range(2, p.chunks)] if p.chunks > 3 else [range(p.chunks)]
 
     def project(f):
         rows = jnp.concatenate([att[f, head] for head in range(p.group)], axis=1)
-        for group in groups:
-            for c in group:
+        for g, (start, length) in enumerate(groups):
+            for c in range(start, start + length):
                 cols = pl.ds(c * p.chunk, p.chunk)
                 product = jnp.dot(rows, weight[:, cols], preferred_element_type=jnp.float32)
                 term[f, c] = product.astype(jnp.bfloat16).reshape(term.shape[2:])
-            for c in group:
-                halving(f, c, 0).start()
+            to_partner(f, g).start()
+
+    def across_x(f, c):
+        return pltpu.make_async_remote_copy(
+            src_ref=landed0.at[f, c, 1 - across],
+            dst_ref=landed1.at[f, c],
+            send_sem=s5,
+            recv_sem=r5.at[f, c],
+            device_id={"head": h + 2 - 4 * across},
+            device_id_type=MESH,
+        )
 
     def pair_sum(f, c):
-        halving(f, c, 0).wait_recv()
+        for g, (start, _) in enumerate(groups):
+            if c == start:
+                to_partner(f, g).wait_recv()
         total = term[f, c, core].astype(jnp.float32) + landed0[f, c].astype(jnp.float32)
         landed0[f, c] = total.astype(jnp.bfloat16)
-        halving(f, c, 1).start()
-
-    def to_owner(f, c, ds, row):
-        to_s = lax.rem(s + ds, p.ns)
-        return pltpu.make_async_remote_copy(
-            src_ref=landed1.at[f, c, to_s],
-            dst_ref=final.at[f, c, row],
-            send_sem=s6.at[ds - 1, f, c],
-            recv_sem=r6.at[ds - 1, f, c],
-            device_id={"seq": to_s},
-            device_id_type=MESH,
-        )
+        across_x(f, c).start()
 
     def full_sum(f, c):
-        halving(f, c, 1).wait_recv()
+        across_x(f, c).wait_recv()
         total = landed0[f, c, across].astype(jnp.float32) + landed1[f, c].astype(jnp.float32)
         landed1[f, c] = total.astype(jnp.bfloat16)
         for ds in (2, 1, 3):
-            to_owner(f, c, ds, s).start()
-        final[f, c, s] = landed1[f, c, s]
-
-    gather(first_part)
+            to_s = lax.rem(s + ds, p.ns)
+            pltpu.make_async_remote_copy(
+                src_ref=landed1.at[f, c, to_s],
+                dst_ref=final.at[f, c, ds - 1],
+                send_sem=s6,
+                recv_sem=r6.at[f, c],
+                device_id={"seq": to_s},
+                device_id_type=MESH,
+            ).start()
+
+    gather(functools.partial(part, 0))
     late[0].wait()
     project(0)
     def pair_sums():
@@ -511,7 +494,7 @@
             pair_sum(0, c)
 
     pl.when(at_end)(pair_sums)
-    gather(second_part)
+    gather(functools.partial(part, 1))
     pl.when(jnp.logical_not(at_end))(pair_sums)
     project(1)
     for c in range(p.chunks):
@@ -523,37 +506,42 @@
         rows_ref[i] = row[...]
 
     def finish(f, c, sums):
-        for ds in range(1, p.ns):
-            to_owner(f, c, ds, lax.rem(s - ds + p.ns, p.ns)).wait_recv()
+        pltpu.make_async_copy(final.at[f, c], final.at[f, c], r6.at[f, c]).wait()
         rows = slice(f * p.cells, (f + 1) * p.cells)
-        for j in range(p.ns):
-            cols = slice(j * p.columns + c * p.chunk, j * p.columns + (c + 1) * p.chunk)
-            added = gate_ref[:, cols] * final[f, c, j].astype(jnp.float32)
+        for ds in range(p.ns):
+            j = lax.rem(s - ds + p.ns, p.ns)
+            cols = pl.ds(pl.multiple_of(j * p.columns + c * p.chunk, 128), p.chunk)
+            part = landed1[f, c, s] if ds == 0 else final[f, c, ds - 1]
+            added = gate_ref[:, cols] * part.astype(jnp.float32)
             value = (res[rows, cols].astype(jnp.float32) + added).astype(jnp.bfloat16)
             hidden_ref[rows, cols] = value
             sums = sums + jnp.sum(value.astype(jnp.float32), -1, keepdims=True)
         return sums
 
+    patch[...] = jnp.zeros_like(patch)
+
+    def head(f, sums):
+        rows = slice(f * p.cells, (f + 1) * p.cells)
+        center = hidden_ref[rows].astype(jnp.float32) - sums / p.width
+        spread = jnp.mean(center * center, -1, keepdims=True)
+        normed = center * lax.rsqrt(spread + 1e-06) * (1.0 + scale_ref[...]) + shift_ref[...]
+        values = lax.dot_general(
+            normed.astype(jnp.bfloat16),
+            head_w[...],
+            (((1,), (1,)), ((), ())),
+            preferred_element_type=jnp.float32,
+        )
+        values = (values + bias_ref[...]).astype(jnp.bfloat16)
+        patch[rows, : values.shape[-1]] = values
+
     sums = [jnp.zeros((p.cells, 1), jnp.float32) for _ in range(p.frames)]
     for c in range(p.chunks):
         full_sum(1, c)
         sums[0] = finish(0, c, sums[0])
+    head(0, sums[0])
     for c in range(p.chunks):
         sums[1] = finish(1, c, sums[1])
-    mean = jnp.concatenate(sums, axis=0) / p.width
-    center = hidden_ref[...].astype(jnp.float32) - mean
-    spread = jnp.mean(center * center, -1, keepdims=True)
-    normed = center * lax.rsqrt(spread + 1e-06) * (1.0 + scale_ref[...]) + shift_ref[...]
-    values = lax.dot_general(
-        normed.astype(jnp.bfloat16),
-        head_w[...],
-        (((1,), (1,)), ((), ())),
-        preferred_element_type=jnp.float32,
-    )
-    values = (values + bias_ref[...]).astype(jnp.bfloat16)
-    features = values.shape[-1]
-    patch[...] = jnp.zeros_like(patch)
-    patch[:, :features] = values
+    head(1, sums[1])
     blank = jnp.zeros(patch.shape, patch.dtype)
 
     moves = [(0, 1), (0, -1), (1, 0), (1, 1), (1, -1)]
@@ -600,24 +588,23 @@
         def _():
             reach(index).wait_send()
 
-    for phase, heads in stages:
-        for_sends(phase, heads, lambda copy: copy.wait_send())
+    def all_sent(part, sem):
+        pltpu.make_async_copy(part, part, sem).wait()
 
     for row in range(p.ns):
         @pl.when(s == row)
         def _():
-            for f in range(p.frames):
-                for head in range(p.group):
-                    for way, to_s in enumerate(targets(head, row)):
-                        for cut in range(p.cuts):
-                            hop(f, head, cut, to_s, way).wait_send()
-
-    for f in range(p.frames):
-        for c in range(p.chunks):
-            for b in range(2):
-                halving(f, c, b).wait_send()
-            for ds in range(1, p.ns):
-                to_owner(f, c, ds, s).wait_send()
+            foreign = (p.nh * p.group - p.counts[row]) * HEAD_DIM
+            all_sent(qkv.at[:, :, :, pl.ds(0, foreign)], s1)
+            for relayed in range(2):
+                heads = [head for head in range(p.group) if (p.owner[head] != row) == relayed]
+                sent = sum(len(targets(head, row)) for head in heads)
+                if sent:
+                    all_sent(att.at[:, pl.ds(0, sent)], s3.at[relayed])
+
+    all_sent(landed0, s4)
+    all_sent(landed1, s5)
+    all_sent(final, s6)
 
 
 def spread_weights(conv_w, wide_ref):
@@ -717,7 +704,6 @@
     t, cells, width, patch_size = p.tokens, p.cells, p.width, head_weight.shape[1]
     dma, bf16 = pltpu.SemaphoreType.DMA, jnp.bfloat16
     lanes = -(-patch_size // 128) * 128
-    most = 2 * p.few * HEAD_DIM
     channels = conv_weight.shape[-1]
     hbm = pl.BlockSpec(memory_space=pltpu.HBM)
     vmem = pl.BlockSpec(memory_space=pltpu.VMEM)
@@ -733,7 +719,7 @@
         out_specs=(vmem,) * 4,
         scratch_shapes=[
             pltpu.VMEM((3, frames, cells, inner), bf16),
-            pltpu.VMEM((3, frames, p.slots, cells, most), bf16),
+            pltpu.VMEM((2, 3, frames, p.slots, cells, p.few * HEAD_DIM), bf16),
             pltpu.VMEM((frames, p.group, p.slots * cells, HEAD_DIM), bf16),
             pltpu.VMEM(out_weight.shape, bf16),
             pltpu.VMEM((t, width), bf16),
@@ -748,18 +734,22 @@
             pltpu.VMEM((frames, p.chunks, 2, 2, ns, cells, p.chunk), bf16),
             pltpu.VMEM((frames, p.chunks, 2, ns, cells, p.chunk), bf16),
             pltpu.VMEM((frames, p.chunks, ns, cells, p.chunk), bf16),
-            pltpu.VMEM((frames, p.chunks, ns, cells, p.chunk), bf16),
+            pltpu.VMEM((frames, p.chunks, ns - 1, cells, p.chunk), bf16),
             pltpu.VMEM((t, lanes), bf16),
             pltpu.VMEM((5, t, lanes), bf16),
-            dma((16,)),
-            dma((3, p.slots - 1)),
-            dma((3, p.slots - 1)),
-            dma((2, frames, p.group, p.cuts)),
+            dma(()),
+            dma((10,)),
+            dma((2,)),
+            dma(()),
+            dma((3,)),
+            dma((2,)),
             dma((frames, p.group, p.cuts)),
-            dma((2, frames, p.chunks)),
-            dma((2, frames, p.chunks)),
-            dma((ns - 1, frames, p.chunks)),
-            dma((ns - 1, frames, p.chunks)),
+            dma(()),
+            dma((frames, 2)),
+            dma(()),
+            dma((frames, p.chunks)),
+            dma(()),
+            dma((frames, p.chunks)),
             dma((5,)),
             dma((5,)),
         ],

time: 54 us -> 51.7 us (0.957)
  Pallas kernels: 53.2 us -> 50.9 us
    pallas_call x1, Pallas kernels: 51.7 us -> 49.4 us  [on_device(): pl.pallas_call(functools.partial(block_kernel, p), out_shape=(jax.ShapeDt...]
where the time goes in v3:
time: 51.7 us; the launch traced here: 51.6 us
  Pallas kernels  50.9 us (98%)
  between operations  0.64 us (1%)
    pallas_call x1, Pallas kernels, on_device(): pl.pallas_call(functools.partial(block_kernel, p), out_shape=(jax.ShapeDt...  49.4 us
    pallas_call x1, Pallas kernels, on_device(): pl.pallas_call(functools.partial(conv_kernel, cells), out_shape=(jax.Shap...  1.5 us

profile of v3, /device:TPU:0, one launch (start us, length us, event | category | flops | bytes accessed | tf_op | source)
XLA Modules:
  0.0 51.6 jit_solution(17899391173978633420)
XLA Ops:
  0.6 49.4 %shard_map.140 = (bf16[32,5120]{1,0:T(8,128)(2,1)S(1)}, bf16[2,3,32,128]{3,2,1,0:T(8,128)(2,1)S(1)}, bf16[2,3,256,768]{3,2,1,0:T(8,128)(2,1)S(1)}, f32[2,384]{1,0:T(2,128)S(1)}) custom-call(bf16[2,16,3072]{2,1,0:T(8,128)(2,1)} %bitcast.16, bf16[2,16,3072]{2,1,0:T(8,128)(2,1)} %bitcast.17, bf16[2,16,3072]{2,1,0:T(8,128)(2,1)} %bitcast.18, ...), custom_call_target="tpu_custom_call" | custom-call | tf_op jit(solution)/shard_map/pallas_call | solution.py:710
  50.1 1.5 %shard_map.141 = (bf16[32,5120]{1,0:T(8,128)(2,1)}, bf16[2,2,32,384]{3,2,1,0:T(8,128)(2,1)}) custom-call(bf16[32,5120]{1,0:T(8,128)(2,1)S(1)} %get-tuple-element.8.hidden_ref, bf16[2,3,32,128]{3,2,1,0:T(8,128)(2,1)S(1)} %get-tuple-element.9.near_ref, bf16[2,3,256,768]{3,2,1,0:T(8,128)(2,1)S(1)} %get-tuple-element.10.wide_ref, ...), custom_call_target="tpu_custom_call" | custom-call | tf_op jit(solution)/shard_map/pallas_call | solution.py:774

commit v4 on v3

--- a/solution.py
+++ b/solution.py
@@ -225,7 +225,7 @@
 def due(o, unit, f, row):
     away = abs(row - o)
     if o in (0, 3):
-        return (0, 15.0, 15.5, 18.5)[away] + 1.5 * f
+        return (0, 15.0, 15.5, 18.5)[away] + 6.5 * f
     if row == 3 * (o // 2):
         return (10.0, 18.0)[unit] + 1.4 * f
     return (15.7, 19.4)[unit] + 3.0 * (away - 1) + 1.4 * f
@@ -245,10 +245,11 @@
     core, across = h & 1, h >> 1
     row_pair = (bias_row, gain_row)
 
-    def slot(seq_index, head_index):
-        return ((head_index & 1) * 2 + (head_index >> 1)) * p.ns + seq_index
-
-    here = slot(s, h)
+    def pair_of(seq_index):
+        return ((seq_index + 1) >> 1) & 1
+
+    place = s >> 1
+    here = ((pair_of(s) * 2 + core) * 2 + across) * 2 + place
     at_end = (s == 0) | (s == p.ns - 1)
     offsets = [(ds, dh) for ds in range(p.ns) for dh in range(p.nh) if ds or dh]
     wide = p.few * HEAD_DIM
@@ -364,154 +365,216 @@
         product = jnp.dot(weights.astype(jnp.bfloat16), v, preferred_element_type=jnp.float32)
         att[f, p.few * jnp.maximum(2 * s - 1, 0) + j] = (product / denominator).astype(jnp.bfloat16)
 
+    parts = [(f, cut) for f in range(p.frames) for cut in range(p.cuts)]
+
     def targets(head, row):
         o = p.owner[head]
         rows = [r for r in range(p.ns) if r != o and source_row(o, r) == row]
         return sorted(rows, key=lambda r: -abs(r - row))
 
-    def send_own(f, j):
+    def send_own(f, j, outward=(True, False)):
         for row in range(p.ns):
             if j < p.counts[row]:
                 head = p.owner.index(row) + j
 
                 @pl.when(s == row)
                 def _():
-                    for to_s in targets(head, row):
-                        for cut in range(p.cuts):
-                            hop(f, head, cut, to_s, 0).start()
+                    rows = [r for r in targets(head, row) if (r in (0, p.ns - 1)) in outward]
+                    pieces = [(cut, to_s) for cut in range(p.cuts) for to_s in rows]
+                    for cut, to_s in pieces:
+                        hop(f, head, cut, to_s, 0).start()
 
     def order(row):
         def when(item):
-            f, head = item
+            f, cut, head = item
             o = p.owner[head]
-            return (f, due(o, (head - p.owner.index(o)) // p.few, f, row), head)
-
-        every = [(f, head) for f in range(p.frames) for head in range(p.group)]
-        return sorted((item for item in every if p.owner[item[1]] != row), key=when)
-
-    def take(f, head, row):
-        for cut in range(p.cuts):
-            hop(f, head, cut, row, 1).wait_recv()
-            for to_s in targets(head, row):
-                hop(f, head, cut, to_s, 1).start()
+            passive = not targets(head, row)
+            return (f, cut, passive, due(o, (head - p.owner.index(o)) // p.few, f, row), head)
+
+        heads = [head for head in range(p.group) if p.owner[head] != row]
+        return sorted(((f, cut, head) for f, cut in parts for head in heads), key=when)
 
     def gather(todo):
         for row in range(p.ns):
             @pl.when(s == row)
             def _():
-                for f, head in todo(row):
-                    take(f, head, row)
+                for f, cut, head in todo(row):
+                    hop(f, head, cut, row, 1).wait_recv()
+                    for to_s in targets(head, row):
+                        hop(f, head, cut, to_s, 1).start()
 
     def early_part(row):
-        def early(f, head):
+        def early(f, cut, head):
             unit = (head - p.owner.index(p.owner[head])) // p.few
             return f == 0 and unit == 0 and row in (1, 2) and targets(head, row)
 
         return [item for item in order(row) if early(*item)]
 
-    def part(f, row):
-        return [item for item in order(row) if item[0] == f and item not in early_part(row)]
+    def first_part(row):
+        if row not in (0, p.ns - 1):
+            return []
+        return [(0, 0, head) for head in range(p.group) if p.owner[head] == (1, 2)[row // 3]]
+
+    def gather_part(f, cut):
+        def todo(row):
+            done = early_part(row) + first_part(row)
+            return [item for item in order(row) if item[:2] == (f, cut) and item not in done]
+
+        gather(todo)
 
     own_copied(0).wait()
     pl.when(at_end)(functools.partial(arrived, 0))
     pl.when(jnp.logical_not(at_end))(functools.partial(arrived, 1))
+    def at_ends(act, *of):
+        pl.when(at_end)(functools.partial(act, *of))
+
+    def at_middle(act, *of):
+        pl.when(jnp.logical_not(at_end))(functools.partial(act, *of))
+
     for f in range(p.frames):
         for j in range(p.few):
             attend(f, j)
-            send_own(f, j)
-
-    @pl.when(jnp.logical_not(at_end))
+            if f == 0:
+                send_own(f, j)
+            else:
+                at_middle(send_own, f, j, (True,))
+
+    @at_middle
     def _():
         own_copied(1).wait()
         arrived(2)
         for f in range(p.frames):
             for j in range(p.few, 2 * p.few):
                 attend(f, j)
-                send_own(f, j)
+                send_own(f, j, (True, False) if f == 0 else (False,))
             if f == 0:
+                for j in range(p.few):
+                    send_own(1, j, (False,))
                 gather(early_part)
 
+    @at_ends
+    def _():
+        gather(first_part)
+        for j in range(p.few):
+            send_own(1, j)
+
     groups = [(0, 2), (2, p.chunks - 2)] if p.chunks > 3 else [(0, p.chunks)]
 
-    def to_partner(f, g):
+    def to_partner(f, cut, g):
         part = pl.ds(*groups[g])
         return pltpu.make_async_remote_copy(
-            src_ref=term.at[f, part, 1 - core],
-            dst_ref=landed0.at[f, part],
+            src_ref=term.at[f, cut, part, 1 - core],
+            dst_ref=landed0.at[f, cut, part],
             send_sem=s4,
-            recv_sem=r4.at[f, g],
+            recv_sem=r4.at[f, cut, g],
             device_id={"head": h + 1 - 2 * core},
             device_id_type=MESH,
         )
 
-    def project(f):
-        rows = jnp.concatenate([att[f, head] for head in range(p.group)], axis=1)
-        for g, (start, length) in enumerate(groups):
-            for c in range(start, start + length):
+    def project(f, cut):
+        length = p.slots * p.cells // p.cuts
+        own = pl.ds(cut * length, length)
+        rows = jnp.concatenate([att[f, head, own] for head in range(p.group)], axis=1)
+        for g, (start, count) in enumerate(groups):
+            for c in range(start, start + count):
                 cols = pl.ds(c * p.chunk, p.chunk)
                 product = jnp.dot(rows, weight[:, cols], preferred_element_type=jnp.float32)
-                term[f, c] = product.astype(jnp.bfloat16).reshape(term.shape[2:])
-            to_partner(f, g).start()
-
-    def across_x(f, c):
+                term[f, cut, c] = product.astype(jnp.bfloat16).reshape(term.shape[3:])
+            to_partner(f, cut, g).start()
+
+    def across_x(f, cut, g):
+        part = pl.ds(*groups[g])
         return pltpu.make_async_remote_copy(
-            src_ref=landed0.at[f, c, 1 - across],
-            dst_ref=landed1.at[f, c],
+            src_ref=landed0.at[f, cut, part, 1 - across],
+            dst_ref=landed1.at[f, cut, part],
             send_sem=s5,
-            recv_sem=r5.at[f, c],
+            recv_sem=r5.at[f, cut, g],
             device_id={"head": h + 2 - 4 * across},
             device_id_type=MESH,
         )
 
-    def pair_sum(f, c):
-        for g, (start, _) in enumerate(groups):
-            if c == start:
-                to_partner(f, g).wait_recv()
-        total = term[f, c, core].astype(jnp.float32) + landed0[f, c].astype(jnp.float32)
-        landed0[f, c] = total.astype(jnp.bfloat16)
-        across_x(f, c).start()
-
-    def full_sum(f, c):
-        across_x(f, c).wait_recv()
-        total = landed0[f, c, across].astype(jnp.float32) + landed1[f, c].astype(jnp.float32)
-        landed1[f, c] = total.astype(jnp.bfloat16)
+    def pair_sum(f, cut, g):
+        part = pl.ds(*groups[g])
+        to_partner(f, cut, g).wait_recv()
+        total = term[f, cut, part, core].astype(jnp.float32)
+        total = total + landed0[f, cut, part].astype(jnp.float32)
+        landed0[f, cut, part] = total.astype(jnp.bfloat16)
+        across_x(f, cut, g).start()
+
+    def full_sum(f, cut, g):
+        part = pl.ds(*groups[g])
+        across_x(f, cut, g).wait_recv()
+        total = landed0[f, cut, part, across].astype(jnp.float32)
+        total = total + landed1[f, cut, part].astype(jnp.float32)
+        landed1[f, cut, part] = total.astype(jnp.bfloat16)
         for ds in (2, 1, 3):
             to_s = lax.rem(s + ds, p.ns)
-            pltpu.make_async_remote_copy(
-                src_ref=landed1.at[f, c, to_s],
-                dst_ref=final.at[f, c, ds - 1],
-                send_sem=s6,
-                recv_sem=r6.at[f, c],
-                device_id={"seq": to_s},
-                device_id_type=MESH,
-            ).start()
-
-    gather(functools.partial(part, 0))
+
+            @pl.when(pair_of(to_s) == cut)
+            def _():
+                pltpu.make_async_remote_copy(
+                    src_ref=landed1.at[f, cut, part, to_s >> 1],
+                    dst_ref=final.at[f, part, ds - 1],
+                    send_sem=s6,
+                    recv_sem=r6.at[f, g],
+                    device_id={"seq": to_s},
+                    device_id_type=MESH,
+                ).start()
+
+    both = range(len(groups))
+
+    def pair_sums(f, cut):
+        for g in both:
+            pair_sum(f, cut, g)
+
+    def full_sums(f, cut):
+        for g in both:
+            full_sum(f, cut, g)
+
+    gather_part(*parts[0])
+    at_middle(gather_part, *parts[1])
+
+    @at_middle
+    def _():
+        for j in range(p.few, 2 * p.few):
+            send_own(1, j, (True,))
+
     late[0].wait()
-    project(0)
-    def pair_sums():
-        for c in range(p.chunks):
-            pair_sum(0, c)
-
-    pl.when(at_end)(pair_sums)
-    gather(functools.partial(part, 1))
-    pl.when(jnp.logical_not(at_end))(pair_sums)
-    project(1)
-    for c in range(p.chunks):
-        pair_sum(1, c)
-        full_sum(0, c)
+    project(*parts[0])
+    at_ends(gather_part, *parts[1])
+    project(*parts[1])
+    pair_sums(*parts[0])
+    at_middle(gather_part, *parts[2])
+    at_middle(gather_part, *parts[3])
+    pair_sums(*parts[1])
+    at_ends(gather_part, *parts[2])
+    project(*parts[2])
+    at_ends(pair_sums, *parts[2])
+    at_ends(full_sums, *parts[0])
+    at_ends(gather_part, *parts[3])
+    project(*parts[3])
+    at_middle(pair_sums, *parts[2])
+    pair_sums(*parts[3])
+    full_sums(*parts[1])
+    at_middle(full_sums, *parts[0])
+    at_middle(full_sums, *parts[3])
+    full_sums(*parts[2])
+    at_ends(full_sums, *parts[3])
     for copy in late[1:]:
         copy.wait()
     for i, row in enumerate(row_pair):
         rows_ref[i] = row[...]
 
     def finish(f, c, sums):
-        pltpu.make_async_copy(final.at[f, c], final.at[f, c], r6.at[f, c]).wait()
+        for g, (start, count) in enumerate(groups):
+            if c == start:
+                pieces = final.at[f, pl.ds(start, count)]
+                pltpu.make_async_copy(pieces, pieces, r6.at[f, g]).wait()
         rows = slice(f * p.cells, (f + 1) * p.cells)
         for ds in range(p.ns):
             j = lax.rem(s - ds + p.ns, p.ns)
             cols = pl.ds(pl.multiple_of(j * p.columns + c * p.chunk, 128), p.chunk)
-            part = landed1[f, c, s] if ds == 0 else final[f, c, ds - 1]
+            part = landed1[f, pair_of(s), c, place] if ds == 0 else final[f, c, ds - 1]
             added = gate_ref[:, cols] * part.astype(jnp.float32)
             value = (res[rows, cols].astype(jnp.float32) + added).astype(jnp.bfloat16)
             hidden_ref[rows, cols] = value
@@ -536,7 +599,6 @@
 
     sums = [jnp.zeros((p.cells, 1), jnp.float32) for _ in range(p.frames)]
     for c in range(p.chunks):
-        full_sum(1, c)
         sums[0] = finish(0, c, sums[0])
     head(0, sums[0])
     for c in range(p.chunks):
@@ -731,9 +793,9 @@
             pltpu.VMEM((9, 3 * conv_weight.shape[3], channels), bf16),
             pltpu.VMEM((channels,), jnp.float32),
             pltpu.VMEM((channels,), jnp.float32),
-            pltpu.VMEM((frames, p.chunks, 2, 2, ns, cells, p.chunk), bf16),
-            pltpu.VMEM((frames, p.chunks, 2, ns, cells, p.chunk), bf16),
-            pltpu.VMEM((frames, p.chunks, ns, cells, p.chunk), bf16),
+            pltpu.VMEM((frames, p.cuts, p.chunks, 2, 2, 2, cells, p.chunk), bf16),
+            pltpu.VMEM((frames, p.cuts, p.chunks, 2, 2, cells, p.chunk), bf16),
+            pltpu.VMEM((frames, p.cuts, p.chunks, 2, cells, p.chunk), bf16),
             pltpu.VMEM((frames, p.chunks, ns - 1, cells, p.chunk), bf16),
             pltpu.VMEM((t, lanes), bf16),
             pltpu.VMEM((5, t, lanes), bf16),
@@ -745,11 +807,11 @@
             dma((2,)),
             dma((frames, p.group, p.cuts)),
             dma(()),
+            dma((frames, p.cuts, 2)),
+            dma(()),
+            dma((frames, p.cuts, 2)),
+            dma(()),
             dma((frames, 2)),
-            dma(()),
-            dma((frames, p.chunks)),
-            dma(()),
-            dma((frames, p.chunks)),
             dma((5,)),
             dma((5,)),
         ],

time: 51.7 us -> 50.1 us (0.969)
  Pallas kernels: 50.9 us -> 49.3 us
    pallas_call x1, Pallas kernels: 49.4 us -> 47.8 us  [on_device(): pl.pallas_call(functools.partial(block_kernel, p), out_shape=(jax.ShapeDt...]
where the time goes in v4:
time: 50.1 us; the launch traced here: 49.9 us
  Pallas kernels  49.3 us (98%)
  between operations  0.64 us (1%)
    pallas_call x1, Pallas kernels, on_device(): pl.pallas_call(functools.partial(block_kernel, p), out_shape=(jax.ShapeDt...  47.8 us
    pallas_call x1, Pallas kernels, on_device(): pl.pallas_call(functools.partial(conv_kernel, cells), out_shape=(jax.Shap...  1.49 us

profile of v4, /device:TPU:0, one launch (start us, length us, event | category | flops | bytes accessed | tf_op | source)
XLA Modules:
  0.0 49.9 jit_solution(8314592380035199952)
XLA Ops:
  0.6 47.8 %shard_map.140 = (bf16[32,5120]{1,0:T(8,128)(2,1)S(1)}, bf16[2,3,32,128]{3,2,1,0:T(8,128)(2,1)S(1)}, bf16[2,3,256,768]{3,2,1,0:T(8,128)(2,1)S(1)}, f32[2,384]{1,0:T(2,128)S(1)}) custom-call(bf16[2,16,3072]{2,1,0:T(8,128)(2,1)} %bitcast.16, bf16[2,16,3072]{2,1,0:T(8,128)(2,1)} %bitcast.17, bf16[2,16,3072]{2,1,0:T(8,128)(2,1)} %bitcast.18, ...), custom_call_target="tpu_custom_call" | custom-call | tf_op jit(solution)/shard_map/pallas_call | solution.py:772
  48.4 1.5 %shard_map.141 = (bf16[32,5120]{1,0:T(8,128)(2,1)}, bf16[2,2,32,384]{3,2,1,0:T(8,128)(2,1)}) custom-call(bf16[32,5120]{1,0:T(8,128)(2,1)S(1)} %get-tuple-element.8.hidden_ref, bf16[2,3,32,128]{3,2,1,0:T(8,128)(2,1)S(1)} %get-tuple-element.9.near_ref, bf16[2,3,256,768]{3,2,1,0:T(8,128)(2,1)S(1)} %get-tuple-element.10.wide_ref, ...), custom_call_target="tpu_custom_call" | custom-call | tf_op jit(solution)/shard_map/pallas_call | solution.py:836

commit v5 on v4

--- a/solution.py
+++ b/solution.py
@@ -225,7 +225,7 @@
 def due(o, unit, f, row):
     away = abs(row - o)
     if o in (0, 3):
-        return (0, 15.0, 15.5, 18.5)[away] + 6.5 * f
+        return (0, 15.0, 16.5, 18.5)[away] + 6.5 * f
     if row == 3 * (o // 2):
         return (10.0, 18.0)[unit] + 1.4 * f
     return (15.7, 19.4)[unit] + 3.0 * (away - 1) + 1.4 * f
@@ -237,7 +237,7 @@
     gate_hbm, shift_hbm, scale_hbm, bias_hbm, cw_hbm, cb_hbm, gain_hbm,
     hidden_ref, near_ref, wide_ref, rows_ref,
     qkv, got, att, weight, res, head_w, gate_ref, shift_ref, scale_ref, bias_ref, conv_w, bias_row, gain_row, term, landed0, landed1, final, patch, halo,
-    load_sem, local_sem, own_sem, s1, r1, s3, r3, s4, r4, s5, r5, s6, r6, s7, r7,
+    far, load_sem, local_sem, own_sem, s1, r1, s3, r3, s4, r4, s5, r5, s6, r6, s7, r7,
 ):
     p = plan
     s = lax.axis_index("seq")
@@ -251,7 +251,6 @@
     place = s >> 1
     here = ((pair_of(s) * 2 + core) * 2 + across) * 2 + place
     at_end = (s == 0) | (s == p.ns - 1)
-    offsets = [(ds, dh) for ds in range(p.ns) for dh in range(p.nh) if ds or dh]
     wide = p.few * HEAD_DIM
 
     def columns_of(seq_index, head_index, unit):
@@ -288,14 +287,22 @@
     for copy in loads:
         copy.start()
 
+    def others(row, to_s):
+        for dh in range(p.nh):
+            if row != to_s or dh:
+                yield lax.rem(h + dh, p.nh)
+
+    def say(sem, **to):
+        pl.semaphore_signal(sem, inc=1, device_id=to, device_id_type=MESH)
+
     barrier = pltpu.get_barrier_semaphore()
-    for ds, dh in offsets:
-        pl.semaphore_signal(
-            barrier,
-            inc=1,
-            device_id={"seq": lax.rem(s + ds, p.ns), "head": lax.rem(h + dh, p.nh)},
-            device_id_type=MESH,
-        )
+    for row in range(p.ns):
+        @pl.when(s == row)
+        def _():
+            for to_s in range(max(row - 1, 0), min(row + 2, p.ns)):
+                for to_h in others(row, to_s):
+                    say(barrier, seq=to_s, head=to_h)
+
     for copy in own_copies(0):
         copy.start()
 
@@ -305,7 +312,6 @@
             copy.start()
 
     loaded.wait()
-    pl.semaphore_wait(barrier, len(offsets))
 
     def exchange(stage, to_s, to_h):
         unit = stage // 2
@@ -318,15 +324,30 @@
             device_id_type=MESH,
         )
 
-    for stage in (1, 0, 2):
-        for ds in range(p.ns):
-            to_s = lax.rem(s + ds, p.ns)
-
-            @pl.when(((to_s == 0) | (to_s == p.ns - 1)) == (stage == 0))
-            def _():
-                for ds2, dh in offsets:
-                    if ds2 == ds:
-                        exchange(stage, to_s, lax.rem(h + dh, p.nh)).start()
+    def send_to(row, stages, away):
+        for stage in stages:
+            for to_s in range(p.ns):
+                if (to_s in (0, p.ns - 1)) == (stage == 0) and abs(to_s - row) in away:
+                    for to_h in others(row, to_s):
+                        exchange(stage, to_s, to_h).start()
+
+    for row in range(p.ns):
+        @pl.when(s == row)
+        def _():
+            beside = [r for r in (row - 1, row + 1) if 0 <= r < p.ns]
+            pl.semaphore_wait(barrier, p.nh * (1 + len(beside)) - 1)
+            if len(beside) == 2:
+                for to_s in beside:
+                    say(far.at[0], seq=to_s)
+            send_to(row, (1, 0), (0, 1))
+            pl.semaphore_wait(far.at[0], 1)
+            if len(beside) == 2:
+                say(far.at[1], seq=3 * (row // 2))
+            send_to(row, (1, 0), (2,))
+            if len(beside) == 1:
+                pl.semaphore_wait(far.at[1], 1)
+                send_to(row, (0,), (3,))
+            send_to(row, (2,), range(p.ns))
 
     def arrived(stage):
         parts = got.at[stage // 2, :, :, pl.ds(0, p.slots - 1)]
@@ -799,6 +820,7 @@
             pltpu.VMEM((frames, p.chunks, ns - 1, cells, p.chunk), bf16),
             pltpu.VMEM((t, lanes), bf16),
             pltpu.VMEM((5, t, lanes), bf16),
+            pltpu.SemaphoreType.REGULAR((2,)),
             dma(()),
             dma((10,)),
             dma((2,)),

time: 50.1 us -> 49.2 us (0.982)
  Pallas kernels: 49.3 us -> 48.4 us
    pallas_call x1, Pallas kernels: 47.8 us -> 46.9 us  [on_device(): pl.pallas_call(functools.partial(block_kernel, p), out_shape=(jax.ShapeDt...]
where the time goes in v5:
time: 49.2 us; the launch traced here: 49 us
  Pallas kernels  48.4 us (98%)
  between operations  0.64 us (1%)
    pallas_call x1, Pallas kernels, on_device(): pl.pallas_call(functools.partial(block_kernel, p), out_shape=(jax.ShapeDt...  46.9 us
    pallas_call x1, Pallas kernels, on_device(): pl.pallas_call(functools.partial(conv_kernel, cells), out_shape=(jax.Shap...  1.5 us

profile of v5, /device:TPU:0, one launch (start us, length us, event | category | flops | bytes accessed | tf_op | source)
XLA Modules:
  0.0 49.0 jit_solution(2212015090026705816)
XLA Ops:
  0.6 46.9 %shard_map.140 = (bf16[32,5120]{1,0:T(8,128)(2,1)S(1)}, bf16[2,3,32,128]{3,2,1,0:T(8,128)(2,1)S(1)}, bf16[2,3,256,768]{3,2,1,0:T(8,128)(2,1)S(1)}, f32[2,384]{1,0:T(2,128)S(1)}) custom-call(bf16[2,16,3072]{2,1,0:T(8,128)(2,1)} %bitcast.16, bf16[2,16,3072]{2,1,0:T(8,128)(2,1)} %bitcast.17, bf16[2,16,3072]{2,1,0:T(8,128)(2,1)} %bitcast.18, ...), custom_call_target="tpu_custom_call" | custom-call | tf_op jit(solution)/shard_map/pallas_call | solution.py:793
  47.5 1.5 %shard_map.141 = (bf16[32,5120]{1,0:T(8,128)(2,1)}, bf16[2,2,32,384]{3,2,1,0:T(8,128)(2,1)}) custom-call(bf16[32,5120]{1,0:T(8,128)(2,1)S(1)} %get-tuple-element.8.hidden_ref, bf16[2,3,32,128]{3,2,1,0:T(8,128)(2,1)S(1)} %get-tuple-element.9.near_ref, bf16[2,3,256,768]{3,2,1,0:T(8,128)(2,1)S(1)} %get-tuple-element.10.wide_ref, ...), custom_call_target="tpu_custom_call" | custom-call | tf_op jit(solution)/shard_map/pallas_call | solution.py:858

commit v6 on v5

--- a/solution.py
+++ b/solution.py
@@ -236,7 +236,7 @@
     q_hbm, k_hbm, v_hbm, res_hbm, w_hbm, hw_hbm,
     gate_hbm, shift_hbm, scale_hbm, bias_hbm, cw_hbm, cb_hbm, gain_hbm,
     hidden_ref, near_ref, wide_ref, rows_ref,
-    qkv, got, att, weight, res, head_w, gate_ref, shift_ref, scale_ref, bias_ref, conv_w, bias_row, gain_row, term, landed0, landed1, final, patch, halo,
+    qkv, got, att, weight, res, head_w, head_t, gate_ref, shift_ref, scale_ref, bias_ref, wide_bias, conv_w, bias_row, gain_row, term, landed0, landed1, final, patch, halo,
     far, load_sem, local_sem, own_sem, s1, r1, s3, r3, s4, r4, s5, r5, s6, r6, s7, r7,
 ):
     p = plan
@@ -263,13 +263,23 @@
     late = [
         pltpu.make_async_copy(w_hbm, weight, local_sem.at[0]),
         pltpu.make_async_copy(res_hbm, res, local_sem.at[1]),
-        pltpu.make_async_copy(hw_hbm, head_w, local_sem.at[2]),
+        pltpu.make_async_copy(head_w, head_w, local_sem.at[2]),
         pltpu.make_async_copy(gate_hbm, gate_ref, local_sem.at[3]),
         pltpu.make_async_copy(shift_hbm, shift_ref, local_sem.at[4]),
         pltpu.make_async_copy(scale_hbm, scale_ref, local_sem.at[5]),
         pltpu.make_async_copy(bias_hbm, bias_ref, local_sem.at[6]),
         pltpu.make_async_copy(cb_hbm, row_pair[0], local_sem.at[7]),
         pltpu.make_async_copy(gain_hbm, row_pair[1], local_sem.at[8]),
+    ]
+    quarter = hw_hbm.shape[0] // 4
+    strips = [
+        pltpu.make_async_copy(
+            hw_hbm.at[pl.ds((2 * a + first) * quarter, count * quarter)],
+            head_w.at[pl.ds((4 * a + place) * quarter, count * quarter)],
+            local_sem.at[2],
+        )
+        for a in range(2)
+        for place, first, count in ((0, 1, 1), (1, 0, 2), (3, 0, 1))
     ]
     conv_load = pltpu.make_async_copy(cw_hbm, conv_w, local_sem.at[9])
 
@@ -354,11 +364,17 @@
         pltpu.make_async_copy(parts, parts, r1.at[stage]).wait()
 
     conv_load.start()
-    for copy in late:
+    for copy in late[:2] + strips + late[3:]:
         copy.start()
     wide_ref[...] = jnp.zeros_like(wide_ref)
     conv_load.wait()
     spread_weights(conv_w, wide_ref)
+    for copy in late:
+        copy.wait()
+    for i, row in enumerate(row_pair):
+        rows_ref[i] = row[...]
+    wide_bias[...] = spread_bias(bias_ref[...])
+    head_t[...] = head_w[...].T
 
     def hop(f, head, cut, to_s, relayed):
         rows = p.slots * p.cells // p.cuts
@@ -372,9 +388,9 @@
             device_id_type=MESH,
         )
 
-    def attend(f, j):
+    def attend(f, j, cuts=slice(None)):
         unit, lanes = j // p.few, pl.ds(j % p.few * HEAD_DIM, HEAD_DIM)
-        q = got[unit, 0, f, :, :, lanes].reshape(-1, HEAD_DIM)
+        q = got[unit, 0, f, cuts, :, lanes].reshape(-1, HEAD_DIM)
         k = got[unit, 1, :, :, :, lanes].reshape(-1, HEAD_DIM)
         v = got[unit, 2, :, :, :, lanes].reshape(-1, HEAD_DIM)
         scores = lax.dot_general(
@@ -384,7 +400,9 @@
         weights = jnp.exp2((scores - jnp.max(scores, -1, keepdims=True)) * scale)
         denominator = jnp.sum(weights, -1, keepdims=True)
         product = jnp.dot(weights.astype(jnp.bfloat16), v, preferred_element_type=jnp.float32)
-        att[f, p.few * jnp.maximum(2 * s - 1, 0) + j] = (product / denominator).astype(jnp.bfloat16)
+        rows = slice((cuts.start or 0) * p.cells, (cuts.stop or p.slots) * p.cells)
+        head = p.few * jnp.maximum(2 * s - 1, 0) + j
+        att[f, head, rows] = (product / denominator).astype(jnp.bfloat16)
 
     parts = [(f, cut) for f in range(p.frames) for cut in range(p.cuts)]
 
@@ -393,7 +411,7 @@
         rows = [r for r in range(p.ns) if r != o and source_row(o, r) == row]
         return sorted(rows, key=lambda r: -abs(r - row))
 
-    def send_own(f, j, outward=(True, False)):
+    def send_own(f, j, outward=(True, False), cuts=range(p.cuts)):
         for row in range(p.ns):
             if j < p.counts[row]:
                 head = p.owner.index(row) + j
@@ -401,9 +419,9 @@
                 @pl.when(s == row)
                 def _():
                     rows = [r for r in targets(head, row) if (r in (0, p.ns - 1)) in outward]
-                    pieces = [(cut, to_s) for cut in range(p.cuts) for to_s in rows]
-                    for cut, to_s in pieces:
-                        hop(f, head, cut, to_s, 0).start()
+                    for cut in cuts:
+                        for to_s in rows:
+                            hop(f, head, cut, to_s, 0).start()
 
     def order(row):
         def when(item):
@@ -464,14 +482,17 @@
     def _():
         own_copied(1).wait()
         arrived(2)
-        for f in range(p.frames):
+        half = p.slots // p.cuts
+        for cut in range(p.cuts):
             for j in range(p.few, 2 * p.few):
-                attend(f, j)
-                send_own(f, j, (True, False) if f == 0 else (False,))
-            if f == 0:
-                for j in range(p.few):
-                    send_own(1, j, (False,))
-                gather(early_part)
+                attend(0, j, slice(cut * half, (cut + 1) * half))
+                send_own(0, j, cuts=(cut,))
+        for j in range(p.few):
+            send_own(1, j, (False,))
+        gather(early_part)
+        for j in range(p.few, 2 * p.few):
+            attend(1, j)
+            send_own(1, j, (False,))
 
     @at_ends
     def _():
@@ -560,7 +581,6 @@
         for j in range(p.few, 2 * p.few):
             send_own(1, j, (True,))
 
-    late[0].wait()
     project(*parts[0])
     at_ends(gather_part, *parts[1])
     project(*parts[1])
@@ -570,10 +590,15 @@
     pair_sums(*parts[1])
     at_ends(gather_part, *parts[2])
     project(*parts[2])
-    at_ends(pair_sums, *parts[2])
-    at_ends(full_sums, *parts[0])
+
+    def third_sums():
+        pair_sums(*parts[2])
+        full_sums(*parts[0])
+
+    pl.when(at_end & (core == 0))(third_sums)
     at_ends(gather_part, *parts[3])
     project(*parts[3])
+    pl.when(at_end & (core == 1))(third_sums)
     at_middle(pair_sums, *parts[2])
     pair_sums(*parts[3])
     full_sums(*parts[1])
@@ -581,11 +606,6 @@
     at_middle(full_sums, *parts[3])
     full_sums(*parts[2])
     at_ends(full_sums, *parts[3])
-    for copy in late[1:]:
-        copy.wait()
-    for i, row in enumerate(row_pair):
-        rows_ref[i] = row[...]
-
     def finish(f, c, sums):
         for g, (start, count) in enumerate(groups):
             if c == start:
@@ -602,21 +622,21 @@
             sums = sums + jnp.sum(value.astype(jnp.float32), -1, keepdims=True)
         return sums
 
-    patch[...] = jnp.zeros_like(patch)
-
     def head(f, sums):
         rows = slice(f * p.cells, (f + 1) * p.cells)
         center = hidden_ref[rows].astype(jnp.float32) - sums / p.width
         spread = jnp.mean(center * center, -1, keepdims=True)
         normed = center * lax.rsqrt(spread + 1e-06) * (1.0 + scale_ref[...]) + shift_ref[...]
-        values = lax.dot_general(
-            normed.astype(jnp.bfloat16),
-            head_w[...],
-            (((1,), (1,)), ((), ())),
-            preferred_element_type=jnp.float32,
-        )
-        values = (values + bias_ref[...]).astype(jnp.bfloat16)
-        patch[rows, : values.shape[-1]] = values
+        values = jnp.dot(
+            normed.astype(jnp.bfloat16), head_t[...], preferred_element_type=jnp.float32
+        )
+        values = (values + wide_bias[...]).astype(jnp.bfloat16).astype(jnp.float32)
+        column = lax.broadcasted_iota(jnp.int32, values.shape, 0)
+        place = lax.broadcasted_iota(jnp.int32, values.shape, 1) % (4 * quarter)
+        left = jnp.where(column == 0, 0.0, pltpu.roll(values, 1, 0))
+        right = jnp.where(column == p.cells - 1, 0.0, pltpu.roll(values, p.cells - 1, 0))
+        strip = jnp.where(place < quarter, left, jnp.where(place < 3 * quarter, values, right))
+        patch[rows] = strip.astype(jnp.bfloat16)
 
     sums = [jnp.zeros((p.cells, 1), jnp.float32) for _ in range(p.frames)]
     for c in range(p.chunks):
@@ -702,35 +722,30 @@
                 wide_ref[a, dt, base + part : base + part + depth, channels:] = tap
 
 
+def spread_bias(bias):
+    size = bias.shape[1]
+    part = size // 4
+    source = lax.broadcasted_iota(jnp.int32, (size, 2 * size), 0)
+    target = lax.broadcasted_iota(jnp.int32, (size, 2 * size), 1)
+    place = target % size
+    moved = jnp.where(place < part, part, jnp.where(place < 3 * part, -part, -3 * part))
+    pick = jnp.where(source == target // size * 2 * part + place + moved, 1.0, 0.0)
+    total, rest = 0.0, bias
+    for _ in range(3):
+        piece = rest.astype(jnp.bfloat16)
+        rest = rest - piece.astype(jnp.float32)
+        total = total + jnp.dot(
+            piece, pick.astype(jnp.bfloat16), preferred_element_type=jnp.float32
+        )
+    return total
+
+
 def conv_kernel(
-    cells, hidden_ref, near_ref, wide_ref, rows_ref, hidden_out, features_out, mixed, features, sems
+    cells, hidden_ref, strip, wide_ref, rows_ref, hidden_out, features_out, mixed, features, sems
 ):
-    tokens = near_ref.shape[2]
-    lanes = near_ref.shape[3]
-    part = lanes // 8
     channels = features.shape[-1]
     hidden_copy = pltpu.make_async_copy(hidden_ref, hidden_out, sems.at[0])
     hidden_copy.start()
-
-    values = near_ref[...].reshape(-1, lanes).astype(jnp.float32)
-    total = values.shape[0]
-    column = lax.broadcasted_iota(jnp.int32, values.shape, 0) % cells
-    left = jnp.where(column == 0, 0.0, pltpu.roll(values, 1, 0))
-    right = jnp.where(column == cells - 1, 0.0, pltpu.roll(values, total - 1, 0))
-
-    source = lax.broadcasted_iota(jnp.int32, (lanes, lanes), 0)
-    target = lax.broadcasted_iota(jnp.int32, (lanes, lanes), 1)
-    upper, place = target // (4 * part), target % (4 * part)
-    start = upper * 2 * part
-
-    def moved(x, low, high, first):
-        pick = (place >= low * part) & (place < high * part)
-        pick = pick & (source == start + place + (first - low) * part)
-        matrix = jnp.where(pick, 1.0, 0.0).astype(jnp.bfloat16)
-        return jnp.dot(x.astype(jnp.bfloat16), matrix, preferred_element_type=jnp.float32)
-
-    strip = moved(left, 0, 1, 1) + moved(values, 1, 3, 0) + moved(right, 3, 4, 0)
-    strip = strip.reshape(2, 3, tokens, lanes).astype(jnp.bfloat16)
 
     def at_time(dt, row):
         if dt == 1:
@@ -786,7 +801,7 @@
     frames, height, breadth, inner = queries.shape
     t, cells, width, patch_size = p.tokens, p.cells, p.width, head_weight.shape[1]
     dma, bf16 = pltpu.SemaphoreType.DMA, jnp.bfloat16
-    lanes = -(-patch_size // 128) * 128
+    lanes = 2 * patch_size
     channels = conv_weight.shape[-1]
     hbm = pl.BlockSpec(memory_space=pltpu.HBM)
     vmem = pl.BlockSpec(memory_space=pltpu.VMEM)
@@ -806,11 +821,13 @@
             pltpu.VMEM((frames, p.group, p.slots * cells, HEAD_DIM), bf16),
             pltpu.VMEM(out_weight.shape, bf16),
             pltpu.VMEM((t, width), bf16),
-            pltpu.VMEM(head_weight.shape[::-1], bf16),
+            pltpu.VMEM((lanes, width), bf16),
+            pltpu.VMEM((width, lanes), bf16),
             pltpu.VMEM((1, width), jnp.float32),
             pltpu.VMEM((1, width), jnp.float32),
             pltpu.VMEM((1, width), jnp.float32),
             pltpu.VMEM((1, patch_size), jnp.float32),
+            pltpu.VMEM((1, lanes), jnp.float32),
             pltpu.VMEM((9, 3 * conv_weight.shape[3], channels), bf16),
             pltpu.VMEM((channels,), jnp.float32),
             pltpu.VMEM((channels,), jnp.float32),

time: 49.2 us -> 48.6 us (0.988)
  Pallas kernels: 48.4 us -> 47.8 us
where the time goes in v6:
time: 48.6 us; the launch traced here: 48.5 us
  Pallas kernels  47.8 us (98%)
  between operations  0.64 us (1%)
    pallas_call x1, Pallas kernels, on_device(): pl.pallas_call(functools.partial(block_kernel, p), out_shape=(jax.ShapeDt...  46.5 us
    pallas_call x1, Pallas kernels, on_device(): pl.pallas_call(functools.partial(conv_kernel, cells), out_shape=(jax.Shap...  1.32 us

profile of v6, /device:TPU:0, one launch (start us, length us, event | category | flops | bytes accessed | tf_op | source)
XLA Modules:
  0.0 48.5 jit_solution(1109409019660512466)
XLA Ops:
  0.6 46.5 %shard_map.140 = (bf16[32,5120]{1,0:T(8,128)(2,1)S(1)}, bf16[2,3,32,128]{3,2,1,0:T(8,128)(2,1)S(1)}, bf16[2,3,256,768]{3,2,1,0:T(8,128)(2,1)S(1)}, f32[2,384]{1,0:T(2,128)S(1)}) custom-call(bf16[2,16,3072]{2,1,0:T(8,128)(2,1)} %bitcast.16, bf16[2,16,3072]{2,1,0:T(8,128)(2,1)} %bitcast.17, bf16[2,16,3072]{2,1,0:T(8,128)(2,1)} %bitcast.18, ...), custom_call_target="tpu_custom_call" | custom-call | tf_op jit(solution)/shard_map/pallas_call | solution.py:808
  47.1 1.3 %shard_map.141 = (bf16[32,5120]{1,0:T(8,128)(2,1)}, bf16[2,2,32,384]{3,2,1,0:T(8,128)(2,1)}) custom-call(bf16[32,5120]{1,0:T(8,128)(2,1)S(1)} %get-tuple-element.8.hidden_ref, bf16[2,3,32,128]{3,2,1,0:T(8,128)(2,1)S(1)} %get-tuple-element.9.strip, bf16[2,3,256,768]{3,2,1,0:T(8,128)(2,1)S(1)} %get-tuple-element.10.wide_ref, ...), custom_call_target="tpu_custom_call" | custom-call | tf_op jit(solution)/shard_map/pallas_call | solution.py:875

commit v7 on v6

--- a/solution.py
+++ b/solution.py
@@ -489,9 +489,10 @@
                 send_own(0, j, cuts=(cut,))
         for j in range(p.few):
             send_own(1, j, (False,))
+        for j in range(p.few, 2 * p.few):
+            attend(1, j)
         gather(early_part)
         for j in range(p.few, 2 * p.few):
-            attend(1, j)
             send_own(1, j, (False,))
 
     @at_ends

time: 48.6 us -> 48.6 us (level)
  no operation moved by 1% of the time
where the time goes in v7:
time: 48.6 us; the launch traced here: 48.5 us
  Pallas kernels  47.8 us (98%)
  between operations  0.64 us (1%)
    pallas_call x1, Pallas kernels, on_device(): pl.pallas_call(functools.partial(block_kernel, p), out_shape=(jax.ShapeDt...  46.5 us
    pallas_call x1, Pallas kernels, on_device(): pl.pallas_call(functools.partial(conv_kernel, cells), out_shape=(jax.Shap...  1.32 us

profile of v7, /device:TPU:0, one launch (start us, length us, event | category | flops | bytes accessed | tf_op | source)
XLA Modules:
  0.0 48.5 jit_solution(6509389261150409995)
XLA Ops:
  0.6 46.5 %shard_map.140 = (bf16[32,5120]{1,0:T(8,128)(2,1)S(1)}, bf16[2,3,32,128]{3,2,1,0:T(8,128)(2,1)S(1)}, bf16[2,3,256,768]{3,2,1,0:T(8,128)(2,1)S(1)}, f32[2,384]{1,0:T(2,128)S(1)}) custom-call(bf16[2,16,3072]{2,1,0:T(8,128)(2,1)} %bitcast.16, bf16[2,16,3072]{2,1,0:T(8,128)(2,1)} %bitcast.17, bf16[2,16,3072]{2,1,0:T(8,128)(2,1)} %bitcast.18, ...), custom_call_target="tpu_custom_call" | custom-call | tf_op jit(solution)/shard_map/pallas_call | solution.py:809
  47.1 1.3 %shard_map.141 = (bf16[32,5120]{1,0:T(8,128)(2,1)}, bf16[2,2,32,384]{3,2,1,0:T(8,128)(2,1)}) custom-call(bf16[32,5120]{1,0:T(8,128)(2,1)S(1)} %get-tuple-element.8.hidden_ref, bf16[2,3,32,128]{3,2,1,0:T(8,128)(2,1)S(1)} %get-tuple-element.9.strip, bf16[2,3,256,768]{3,2,1,0:T(8,128)(2,1)S(1)} %get-tuple-element.10.wide_ref, ...), custom_call_target="tpu_custom_call" | custom-call | tf_op jit(solution)/shard_map/pallas_call | solution.py:876
